TPU v7x, 1024 devices: a whole 4x8x16 slice. The times are simulated.
1024 devices in a mesh: block: 64 (over z_lo, y, core), sub: 16 (over z_hi, x).
Axes of the slice: x: 4, y: 8, z: 16 (z_hi: 4, z_lo: 4; z = z_hi * 4 + z_lo), core: 2. Of those that a mesh axis runs over, the one named last changes fastest.
Arguments:
- source: float32 [64, 64, 128, 128], P('block', 'sub'), may hold values from -48 to 48
- trans_x: float32 [64, 64, 128, 128], P('block', 'sub'), may hold values from 0.1 to 10
- trans_y: float32 [64, 64, 128, 128], P('block', 'sub'), may hold values from 0.1 to 10
- trans_z: float32 [64, 64, 128, 128], P('block', 'sub'), may hold values from 0.1 to 10
- mortar_bot: float32 [64, 64, 128, 256], P('block', 'sub'), may hold values from -0.375 to 0.375
- mortar_top: float32 [64, 64, 128, 256], P('block', 'sub'), may hold values from -0.375 to 0.375
Outputs:
- pressure: float32 [64, 64, 128, 128], P('block', 'sub')
- mortar: float32 [64, 256], P('block', 'sub')
All inputs are finite; a program needn't handle non-finite values.
Results may differ from a plain program's by a relative error of at most 0.0003.
Values sent between devices are 32-bit elements; how exact they have to be, the bound alone decides.
A program may use at most 32 MiB of HBM per device.

v0:
```python
import jax
import jax.numpy as jnp
from jax import lax
from jax.sharding import PartitionSpec as P

PASSES = 3
OUTER = 2


RELAX = 0.8
MORTAR_STEP = 0.05
HIGHEST = lax.Precision.HIGHEST


def from_behind(block, axis, distance):
    devices = range(lax.axis_size(axis))
    route = [(i - distance, i) for i in devices if i - distance in devices]
    return lax.ppermute(block, axis, route)


def with_halo(value, sides, width):
    for axis, dim in sides:
        devices, length = (lax.axis_size(axis), value.shape[dim])
        up = [(i, (i + 1) % devices) for i in range(devices - 1)]
        down = [(j, i) for i, j in up]
        last = lax.slice_in_dim(value, length - width, length, axis=dim)
        leading = lax.slice_in_dim(value, 0, width, axis=dim)
        before = lax.ppermute(last, axis, up)
        after = lax.ppermute(leading, axis, down)
        value = jnp.concatenate([before, value, after], axis=dim)
    return value


def from_everyone(value, axis):
    copies = jnp.broadcast_to(value, (lax.axis_size(axis), *value.shape))
    return lax.all_to_all(copies, axis, split_axis=0, concat_axis=0, tiled=True)


def taken_together(value, axis):
    everything = from_everyone(value, axis)
    return jnp.sum(everything, axis=0)


def below_of(values, axis):
    widths = [(0, 0)] * values.ndim
    widths[axis] = (1, 0)
    return lax.slice_in_dim(jnp.pad(values, widths), 0, values.shape[axis], axis=axis)


def above_of(values, axis):
    widths = [(0, 0)] * values.ndim
    widths[axis] = (0, 1)
    return lax.slice_in_dim(jnp.pad(values, widths), 1, values.shape[axis] + 1, axis=axis)


def widen_one(values):
    return jnp.pad(values, ((0, 0), (1, 1), (0, 0), (0, 0)))


def relax_pass(padded, rhs_part, offset, coeffs):
    coupling_x, coupling_next, coupling_y, coupling_z, diagonal = coeffs
    count = padded.shape[1] - 2

    def window(values):
        return values[:, offset : offset + count]

    centre = padded[:, 1:-1]
    part_x = window(coupling_x)
    part_next = window(coupling_next)
    part_y = window(coupling_y)
    part_z = window(coupling_z)
    part_diag = window(diagonal)
    applied = (
        part_diag * centre
        - part_x * padded[:, :-2]
        - part_next * padded[:, 2:]
        - part_y * below_of(centre, 2)
        - above_of(part_y, 2) * above_of(centre, 2)
        - part_z * below_of(centre, 3)
        - above_of(part_z, 3) * above_of(centre, 3)
    )
    return centre + RELAX * (rhs_part - applied) / part_diag


def shards(source, trans_x, trans_y, trans_z, mortar_bot, mortar_top):
    local_x = source.shape[1]
    rows_y = source.shape[2]
    cells_z = source.shape[3]
    mortars = mortar_bot.shape[3]
    sub_count = lax.axis_size("sub")
    block_count = lax.axis_size("block")
    sub_index = lax.axis_index("sub")
    block_index = lax.axis_index("block")
    share = mortars // sub_count
    depth = 1
    global_x = lax.broadcasted_iota(jnp.int32, source.shape, 1) + sub_index * local_x
    masked_x = jnp.where(global_x > 0, trans_x, 0.0)
    upper_layer = from_behind(masked_x[:, 0:1], "sub", -1)
    coupling_x = widen_one(masked_x)
    coupling_next = widen_one(jnp.concatenate([masked_x[:, 1:], upper_layer], axis=1))
    raw_y = widen_one(trans_y)
    raw_z = widen_one(trans_z)
    wide_shape = coupling_x.shape
    wide_x = lax.broadcasted_iota(jnp.int32, wide_shape, 1) - depth + sub_index * local_x
    index_y = lax.broadcasted_iota(jnp.int32, wide_shape, 2)
    index_z = lax.broadcasted_iota(jnp.int32, wide_shape, 3)
    coupling_y = jnp.where(index_y > 0, raw_y, 0.0)
    coupling_z = jnp.where(index_z > 0, raw_z, 0.0)
    dirichlet_bot = jnp.where((index_z == 0) & (block_index > 0), raw_z, 0.0)
    dirichlet_top = jnp.where(
        (index_z == cells_z - 1) & (block_index < block_count - 1), raw_z, 0.0
    )
    diagonal = (
        coupling_x
        + coupling_next
        + coupling_y
        + above_of(coupling_y, 2)
        + coupling_z
        + above_of(coupling_z, 3)
        + dirichlet_bot
        + dirichlet_top
    )
    inside = (wide_x >= 0) & (wide_x < local_x * sub_count)
    diagonal = jnp.where(inside, diagonal, 1.0)
    coeffs = (coupling_x, coupling_next, coupling_y, coupling_z, diagonal)
    local_bot = dirichlet_bot[:, depth : depth + local_x]
    local_top = dirichlet_top[:, depth : depth + local_x]
    face_bot = mortar_bot.reshape(local_x * rows_y, mortars)
    face_top = mortar_top.reshape(local_x * rows_y, mortars)
    pressure = jnp.zeros_like(source)
    mortar_pair = jnp.zeros((2, mortars), jnp.float32)
    final_row = jnp.zeros((share,), jnp.float32)
    for outer_round in range(OUTER):
        bottom_data = jnp.dot(face_bot, mortar_pair[0], precision=HIGHEST).reshape(
            1, local_x, rows_y
        )
        top_data = jnp.dot(face_top, mortar_pair[1], precision=HIGHEST).reshape(1, local_x, rows_y)
        rhs = source + local_bot * bottom_data[..., None] + local_top * top_data[..., None]
        for pass_round in range(PASSES):
            padded = with_halo(pressure, (("sub", 1),), 1)
            pressure = relax_pass(padded, rhs, 1, coeffs)
        flux_bot = local_bot[..., 0] * (pressure[..., 0] - bottom_data)
        flux_top = local_top[..., cells_z - 1] * (pressure[..., cells_z - 1] - top_data)
        terms = jnp.stack(
            [
                jnp.dot(flux_bot.reshape(-1), face_bot, precision=HIGHEST),
                jnp.dot(flux_top.reshape(-1), face_top, precision=HIGHEST),
            ]
        )
        shares = taken_together(terms, "sub")
        current_pair = mortar_pair
        nearby = with_halo(shares[None], (("block", 0),), 1)
        jumps = jnp.stack([nearby[0, 1] + nearby[1, 0], nearby[1, 1] + nearby[2, 0]])
        updated = current_pair + MORTAR_STEP * jumps
        mortar_pair = updated
        final_row = lax.dynamic_slice_in_dim(updated[1], sub_index * share, share, 0)
    return (pressure, final_row[None])


def solution(mesh):
    return jax.shard_map(
        shards,
        mesh=mesh,
        in_specs=(
            P("block", "sub", None, None),
            P("block", "sub", None, None),
            P("block", "sub", None, None),
            P("block", "sub", None, None),
            P("block", "sub", None, None),
            P("block", "sub", None, None),
        ),
        out_specs=(P("block", "sub", None, None), P("block", "sub")),
        check_vma=False,
    )
```

profile of v0, /device:TPU:64, one launch (start us, length us, event | category | flops | bytes accessed | tf_op | source)
XLA Modules:
  0.0 189.7 jit_solution(7265058571942634920)
XLA Ops:
  0.7 1.4 collective-permute-start.2
  2.1 4.5 %collective-permute-start.1 = (f32[1,1,128,128]{2,1,3,0:T(1,128)S(1)}, f32[1,1,128,128]{2,1,3,0:T(1,128)S(1)}, u32[]{:S(2)}, u32[]{:S(2)}) collective-permute-start(f32[1,1,128,128]{2,1,3,0:T(1,128)S(1)} %broadcast.138), channel_id=1, source_target_pairs={{0,1},{1,2},{2,3},{3,4},{4,5},{5,6},{6,7},{7,8},{8,9},{9,10},{10,1... | collective-permute-start | bytes 196616 | tf_op jit(solution)/shard_map/ppermute | solution.py:28
  8.0 1.3 collective-permute-start
  16.7 3.5 %collective-permute-start.3 = (f32[1,1,128,128]{2,1,3,0:T(1,128)S(1)}, f32[1,1,128,128]{2,1,3,0:T(1,128)S(1)}, u32[]{:S(2)}, u32[]{:S(2)}) collective-permute-start(f32[1,1,128,128]{2,1,3,0:T(1,128)S(1)} %get-tuple-element.27), channel_id=1, source_target_pairs={{0,1},{1,2},{2,3},{3,4},{4,5},{5,6},{6,7},{7,8},{8,9},{9,10},{10,1... | collective-permute-start | bytes 196616 | tf_op jit(solution)/shard_map/ppermute | solution.py:28
  20.2 1.3 collective-permute-start.4
  22.1 9.8 %collective-permute-done.4 = f32[1,1,128,128]{2,1,3,0:T(1,128)S(1)} collective-permute-done((f32[1,1,128,128]{2,1,3,0:T(1,128)S(1)}, f32[1,1,128,128]{2,1,3,0:T(1,128)S(1)}, u32[]{:S(2)}, u32[]{:S(2)}) %collective-permute-start.4) | collective-permute-done | bytes 65568 | tf_op jit(solution)/shard_map/ppermute | solution.py:29
  32.8 10.6 %collective-permute-start.5 = (f32[1,1,128,128]{2,1,3,0:T(1,128)S(1)}, f32[1,1,128,128]{2,1,3,0:T(1,128)S(1)}, u32[]{:S(2)}, u32[]{:S(2)}) collective-permute-start(f32[1,1,128,128]{2,1,3,0:T(1,128)S(1)} %get-tuple-element.25), channel_id=1, source_target_pairs={{0,1},{1,2},{2,3},{3,4},{4,5},{5,6},{6,7},{7,8},{8,9},{9,10},{10,1... | collective-permute-start | bytes 196616 | tf_op jit(solution)/shard_map/ppermute | solution.py:28
  43.4 1.3 collective-permute-start.6
  45.3 4.3 %collective-permute-done.6 = f32[1,1,128,128]{2,1,3,0:T(1,128)S(1)} collective-permute-done((f32[1,1,128,128]{2,1,3,0:T(1,128)S(1)}, f32[1,1,128,128]{2,1,3,0:T(1,128)S(1)}, u32[]{:S(2)}, u32[]{:S(2)}) %collective-permute-start.6) | collective-permute-done | bytes 65568 | tf_op jit(solution)/shard_map/ppermute | solution.py:29
  51.2 46.7 %all_to_all.10 = f32[16,2,256]{2,1,0:T(2,128)S(1)} all-to-all(f32[16,2,256]{2,1,0:T(2,128)S(1)} %broadcast_in_dim.31), channel_id=1, replica_groups=mesh['block'=64,'sub'=16] {'sub'}, dimensions={0} | all-to-all | bytes 65536 | tf_op jit(solution)/shard_map/all_to_all | solution.py:36
  97.9 1.9 %collective-permute-start.8 = (f32[1,2,256]{2,1,0:T(2,128)S(1)}, f32[1,2,256]{2,1,0:T(2,128)S(1)}, u32[]{:S(2)}, u32[]{:S(2)}) collective-permute-start(f32[1,2,256]{2,1,0:T(2,128)S(1)} %bitcast.113), channel_id=1, source_target_pairs={{16,0},{32,16},{48,32},{64,48},{80,64},{96,80},{112,96},{128,112},... | collective-permute-start | bytes 6152 | tf_op jit(solution)/shard_map/ppermute | solution.py:29
  99.8 2.4 %collective-permute-start.7 = (f32[1,2,256]{2,1,0:T(2,128)S(1)}, f32[1,2,256]{2,1,0:T(2,128)S(1)}, u32[]{:S(2)}, u32[]{:S(2)}) collective-permute-start(f32[1,2,256]{2,1,0:T(2,128)S(1)} %bitcast.114), channel_id=1, source_target_pairs={{0,16},{16,32},{32,48},{48,64},{64,80},{80,96},{96,112},{112,128},... | collective-permute-start | bytes 6152 | tf_op jit(solution)/shard_map/ppermute | solution.py:28
  102.3 2.5 %collective-permute-start.9 = (f32[1,1,128,128]{2,1,3,0:T(1,128)S(1)}, f32[1,1,128,128]{2,1,3,0:T(1,128)S(1)}, u32[]{:S(2)}, u32[]{:S(2)}) collective-permute-start(f32[1,1,128,128]{2,1,3,0:T(1,128)S(1)} %get-tuple-element.23), channel_id=1, source_target_pairs={{0,1},{1,2},{2,3},{3,4},{4,5},{5,6},{6,7},{7,8},{8,9},{9,10},{10,1... | collective-permute-start | bytes 196616 | tf_op jit(solution)/shard_map/ppermute | solution.py:28
  104.8 1.3 collective-permute-start.10
  106.1 2.8 %collective-permute-done.7 = f32[1,2,256]{2,1,0:T(2,128)S(1)} collective-permute-done((f32[1,2,256]{2,1,0:T(2,128)S(1)}, f32[1,2,256]{2,1,0:T(2,128)S(1)}, u32[]{:S(2)}, u32[]{:S(2)}) %collective-permute-start.7) | collective-permute-done | bytes 2080 | tf_op jit(solution)/shard_map/ppermute | solution.py:28
  109.9 1.7 collective-permute-done.10
  112.6 2.6 %collective-permute-start.11 = (f32[1,1,128,128]{2,1,3,0:T(1,128)S(1)}, f32[1,1,128,128]{2,1,3,0:T(1,128)S(1)}, u32[]{:S(2)}, u32[]{:S(2)}) collective-permute-start(f32[1,1,128,128]{2,1,3,0:T(1,128)S(1)} %get-tuple-element.19), channel_id=1, source_target_pairs={{0,1},{1,2},{2,3},{3,4},{4,5},{5,6},{6,7},{7,8},{8,9},{9,10},{10,1... | collective-permute-start | bytes 196616 | tf_op jit(solution)/shard_map/ppermute | solution.py:28
  117.1 4.3 %collective-permute-done.12 = f32[1,1,128,128]{2,1,3,0:T(1,128)S(1)} collective-permute-done((f32[1,1,128,128]{2,1,3,0:T(1,128)S(1)}, f32[1,1,128,128]{2,1,3,0:T(1,128)S(1)}, u32[]{:S(2)}, u32[]{:S(2)}) %collective-permute-start.12) | collective-permute-done | bytes 65568 | tf_op jit(solution)/shard_map/ppermute | solution.py:29
  122.3 11.3 %collective-permute-start.13 = (f32[1,1,128,128]{2,1,3,0:T(1,128)S(1)}, f32[1,1,128,128]{2,1,3,0:T(1,128)S(1)}, u32[]{:S(2)}, u32[]{:S(2)}) collective-permute-start(f32[1,1,128,128]{2,1,3,0:T(1,128)S(1)} %get-tuple-element.17), channel_id=1, source_target_pairs={{0,1},{1,2},{2,3},{3,4},{4,5},{5,6},{6,7},{7,8},{8,9},{9,10},{10,1... | collective-permute-start | bytes 196616 | tf_op jit(solution)/shard_map/ppermute | solution.py:28
  135.5 4.3 %collective-permute-done.14 = f32[1,1,128,128]{2,1,3,0:T(1,128)S(1)} collective-permute-done((f32[1,1,128,128]{2,1,3,0:T(1,128)S(1)}, f32[1,1,128,128]{2,1,3,0:T(1,128)S(1)}, u32[]{:S(2)}, u32[]{:S(2)}) %collective-permute-start.14) | collective-permute-done | bytes 65568 | tf_op jit(solution)/shard_map/ppermute | solution.py:29
  141.3 34.1 %all_to_all.11 = f32[16,2,256]{2,1,0:T(2,128)S(1)} all-to-all(f32[16,2,256]{2,1,0:T(2,128)S(1)} %broadcast_in_dim.33), channel_id=1, replica_groups=mesh['block'=64,'sub'=16] {'sub'}, dimensions={0} | all-to-all | bytes 65536 | tf_op jit(solution)/shard_map/all_to_all | solution.py:36
  175.4 6.7 %collective-permute-start.16 = (f32[1,2,256]{2,1,0:T(2,128)S(1)}, f32[1,2,256]{2,1,0:T(2,128)S(1)}, u32[]{:S(2)}, u32[]{:S(2)}) collective-permute-start(f32[1,2,256]{2,1,0:T(2,128)S(1)} %bitcast.110), channel_id=1, source_target_pairs={{16,0},{32,16},{48,32},{64,48},{80,64},{96,80},{112,96},{128,112},... | collective-permute-start | bytes 6152 | tf_op jit(solution)/shard_map/ppermute | solution.py:29
  182.1 1.9 %collective-permute-start.15 = (f32[1,2,256]{2,1,0:T(2,128)S(1)}, f32[1,2,256]{2,1,0:T(2,128)S(1)}, u32[]{:S(2)}, u32[]{:S(2)}) collective-permute-start(f32[1,2,256]{2,1,0:T(2,128)S(1)} %bitcast.111), channel_id=1, source_target_pairs={{0,16},{16,32},{32,48},{48,64},{64,80},{80,96},{96,112},{112,128},... | collective-permute-start | bytes 6152 | tf_op jit(solution)/shard_map/ppermute | solution.py:28
  184.9 4.2 %collective-permute-done.15 = f32[1,2,256]{2,1,0:T(2,128)S(1)} collective-permute-done((f32[1,2,256]{2,1,0:T(2,128)S(1)}, f32[1,2,256]{2,1,0:T(2,128)S(1)}, u32[]{:S(2)}, u32[]{:S(2)}) %collective-permute-start.15) | collective-permute-done | bytes 2080 | tf_op jit(solution)/shard_map/ppermute | solution.py:28
  (83 shorter events, 22.1 us)
Async XLA Ops:
  0.6 9.4 %copy-start = (f32[1,4,128,256]{3,2,1,0:T(8,128)S(1)}, f32[1,4,128,256]{3,2,1,0:T(8,128)}, u32[]{:S(2)}) copy-start(f32[1,4,128,256]{3,2,1,0:T(8,128)} %param.10) | copy-start | bytes 1572868
  0.7 14.8 %collective-permute-start.2 = (f32[1,1,128,128]{2,1,3,0:T(1,128)S(1)}, f32[1,1,128,128]{2,1,3,0:T(1,128)S(1)}, u32[]{:S(2)}, u32[]{:S(2)}) collective-permute-start(f32[1,1,128,128]{2,1,3,0:T(1,128)S(1)} %broadcast.138), channel_id=1, source_target_pairs={{1,0},{2,1},{3,2},{4,3},{5,4},{6,5},{7,6},{8,7},{9,8},{10,9},{11,1... | collective-permute-start | bytes 196616 | tf_op jit(solution)/shard_map/ppermute | solution.py:29
  2.1 13.4 %collective-permute-start.1 = (f32[1,1,128,128]{2,1,3,0:T(1,128)S(1)}, f32[1,1,128,128]{2,1,3,0:T(1,128)S(1)}, u32[]{:S(2)}, u32[]{:S(2)}) collective-permute-start(f32[1,1,128,128]{2,1,3,0:T(1,128)S(1)} %broadcast.138), channel_id=1, source_target_pairs={{0,1},{1,2},{2,3},{3,4},{4,5},{5,6},{6,7},{7,8},{8,9},{9,10},{10,1... | collective-permute-start | bytes 196616 | tf_op jit(solution)/shard_map/ppermute | solution.py:28
  7.8 1.7 copy-start.1
  8.0 6.2 %collective-permute-start = (f32[1,1,128,128]{2,1,3,0:T(1,128)S(1)}, f32[1,1,128,128]{2,1,3,0:T(1,128)S(1)}, u32[]{:S(2)}, u32[]{:S(2)}) collective-permute-start(f32[1,1,128,128]{2,1,3,0:T(1,128)S(1)} %slice.352), channel_id=1, source_target_pairs={{1,0},{2,1},{3,2},{4,3},{5,4},{6,5},{7,6},{8,7},{9,8},{10,9},{11,1... | collective-permute-start | bytes 196616 | tf_op jit(solution)/shard_map/ppermute | solution.py:18
  10.0 1.0 copy-start.6
  15.1 35.3 %copy-start.2 = (f32[1,6,128,128]{2,1,3,0:T(8,128)}, f32[1,6,128,128]{2,1,3,0:T(8,128)S(1)}, u32[]{:S(2)}) copy-start(f32[1,6,128,128]{2,1,3,0:T(8,128)S(1)} %get-tuple-element.29) | copy-start | bytes 1179652
  15.1 35.3 %copy-start.4 = (f32[1,6,128,128]{2,1,3,0:T(8,128)}, f32[1,6,128,128]{2,1,3,0:T(8,128)S(1)}, u32[]{:S(2)}) copy-start(f32[1,6,128,128]{2,1,3,0:T(8,128)S(1)} %get-tuple-element.30) | copy-start | bytes 1179652
  16.7 5.4 %collective-permute-start.3 = (f32[1,1,128,128]{2,1,3,0:T(1,128)S(1)}, f32[1,1,128,128]{2,1,3,0:T(1,128)S(1)}, u32[]{:S(2)}, u32[]{:S(2)}) collective-permute-start(f32[1,1,128,128]{2,1,3,0:T(1,128)S(1)} %get-tuple-element.27), channel_id=1, source_target_pairs={{0,1},{1,2},{2,3},{3,4},{4,5},{5,6},{6,7},{7,8},{8,9},{9,10},{10,1... | collective-permute-start | bytes 196616 | tf_op jit(solution)/shard_map/ppermute | solution.py:28
  20.2 11.7 %collective-permute-start.4 = (f32[1,1,128,128]{2,1,3,0:T(1,128)S(1)}, f32[1,1,128,128]{2,1,3,0:T(1,128)S(1)}, u32[]{:S(2)}, u32[]{:S(2)}) collective-permute-start(f32[1,1,128,128]{2,1,3,0:T(1,128)S(1)} %get-tuple-element.28), channel_id=1, source_target_pairs={{1,0},{2,1},{3,2},{4,3},{5,4},{6,5},{7,6},{8,7},{9,8},{10,9},{11,1... | collective-permute-start | bytes 196616 | tf_op jit(solution)/shard_map/ppermute | solution.py:29
  32.8 12.5 %collective-permute-start.5 = (f32[1,1,128,128]{2,1,3,0:T(1,128)S(1)}, f32[1,1,128,128]{2,1,3,0:T(1,128)S(1)}, u32[]{:S(2)}, u32[]{:S(2)}) collective-permute-start(f32[1,1,128,128]{2,1,3,0:T(1,128)S(1)} %get-tuple-element.25), channel_id=1, source_target_pairs={{0,1},{1,2},{2,3},{3,4},{4,5},{5,6},{6,7},{7,8},{8,9},{9,10},{10,1... | collective-permute-start | bytes 196616 | tf_op jit(solution)/shard_map/ppermute | solution.py:28
  43.4 6.2 %collective-permute-start.6 = (f32[1,1,128,128]{2,1,3,0:T(1,128)S(1)}, f32[1,1,128,128]{2,1,3,0:T(1,128)S(1)}, u32[]{:S(2)}, u32[]{:S(2)}) collective-permute-start(f32[1,1,128,128]{2,1,3,0:T(1,128)S(1)} %get-tuple-element.26), channel_id=1, source_target_pairs={{1,0},{2,1},{3,2},{4,3},{5,4},{6,5},{7,6},{8,7},{9,8},{10,9},{11,1... | collective-permute-start | bytes 196616 | tf_op jit(solution)/shard_map/ppermute | solution.py:29
  97.9 8.2 %collective-permute-start.8 = (f32[1,2,256]{2,1,0:T(2,128)S(1)}, f32[1,2,256]{2,1,0:T(2,128)S(1)}, u32[]{:S(2)}, u32[]{:S(2)}) collective-permute-start(f32[1,2,256]{2,1,0:T(2,128)S(1)} %bitcast.113), channel_id=1, source_target_pairs={{16,0},{32,16},{48,32},{64,48},{80,64},{96,80},{112,96},{128,112},... | collective-permute-start | bytes 6152 | tf_op jit(solution)/shard_map/ppermute | solution.py:29
  99.8 9.1 %collective-permute-start.7 = (f32[1,2,256]{2,1,0:T(2,128)S(1)}, f32[1,2,256]{2,1,0:T(2,128)S(1)}, u32[]{:S(2)}, u32[]{:S(2)}) collective-permute-start(f32[1,2,256]{2,1,0:T(2,128)S(1)} %bitcast.114), channel_id=1, source_target_pairs={{0,16},{16,32},{32,48},{48,64},{64,80},{80,96},{96,112},{112,128},... | collective-permute-start | bytes 6152 | tf_op jit(solution)/shard_map/ppermute | solution.py:28
  102.3 7.6 %collective-permute-start.9 = (f32[1,1,128,128]{2,1,3,0:T(1,128)S(1)}, f32[1,1,128,128]{2,1,3,0:T(1,128)S(1)}, u32[]{:S(2)}, u32[]{:S(2)}) collective-permute-start(f32[1,1,128,128]{2,1,3,0:T(1,128)S(1)} %get-tuple-element.23), channel_id=1, source_target_pairs={{0,1},{1,2},{2,3},{3,4},{4,5},{5,6},{6,7},{7,8},{8,9},{9,10},{10,1... | collective-permute-start | bytes 196616 | tf_op jit(solution)/shard_map/ppermute | solution.py:28
  104.8 6.8 %collective-permute-start.10 = (f32[1,1,128,128]{2,1,3,0:T(1,128)S(1)}, f32[1,1,128,128]{2,1,3,0:T(1,128)S(1)}, u32[]{:S(2)}, u32[]{:S(2)}) collective-permute-start(f32[1,1,128,128]{2,1,3,0:T(1,128)S(1)} %get-tuple-element.24), channel_id=1, source_target_pairs={{1,0},{2,1},{3,2},{4,3},{5,4},{6,5},{7,6},{8,7},{9,8},{10,9},{11,1... | collective-permute-start | bytes 196616 | tf_op jit(solution)/shard_map/ppermute | solution.py:29
  108.9 2.7 %copy-start.3 = (f32[1,6,128,128]{2,1,3,0:T(8,128)S(1)}, f32[1,6,128,128]{2,1,3,0:T(8,128)}, u32[]{:S(2)}) copy-start(f32[1,6,128,128]{2,1,3,0:T(8,128)} %copy-done.2) | copy-start | bytes 1179652
  108.9 2.7 %copy-start.5 = (f32[1,6,128,128]{2,1,3,0:T(8,128)S(1)}, f32[1,6,128,128]{2,1,3,0:T(8,128)}, u32[]{:S(2)}) copy-start(f32[1,6,128,128]{2,1,3,0:T(8,128)} %copy-done.4) | copy-start | bytes 1179652
  112.6 4.5 %collective-permute-start.11 = (f32[1,1,128,128]{2,1,3,0:T(1,128)S(1)}, f32[1,1,128,128]{2,1,3,0:T(1,128)S(1)}, u32[]{:S(2)}, u32[]{:S(2)}) collective-permute-start(f32[1,1,128,128]{2,1,3,0:T(1,128)S(1)} %get-tuple-element.19), channel_id=1, source_target_pairs={{0,1},{1,2},{2,3},{3,4},{4,5},{5,6},{6,7},{7,8},{8,9},{9,10},{10,1... | collective-permute-start | bytes 196616 | tf_op jit(solution)/shard_map/ppermute | solution.py:28
  115.2 6.2 %collective-permute-start.12 = (f32[1,1,128,128]{2,1,3,0:T(1,128)S(1)}, f32[1,1,128,128]{2,1,3,0:T(1,128)S(1)}, u32[]{:S(2)}, u32[]{:S(2)}) collective-permute-start(f32[1,1,128,128]{2,1,3,0:T(1,128)S(1)} %get-tuple-element.20), channel_id=1, source_target_pairs={{1,0},{2,1},{3,2},{4,3},{5,4},{6,5},{7,6},{8,7},{9,8},{10,9},{11,1... | collective-permute-start | bytes 196616 | tf_op jit(solution)/shard_map/ppermute | solution.py:29
  122.3 13.2 %collective-permute-start.13 = (f32[1,1,128,128]{2,1,3,0:T(1,128)S(1)}, f32[1,1,128,128]{2,1,3,0:T(1,128)S(1)}, u32[]{:S(2)}, u32[]{:S(2)}) collective-permute-start(f32[1,1,128,128]{2,1,3,0:T(1,128)S(1)} %get-tuple-element.17), channel_id=1, source_target_pairs={{0,1},{1,2},{2,3},{3,4},{4,5},{5,6},{6,7},{7,8},{8,9},{9,10},{10,1... | collective-permute-start | bytes 196616 | tf_op jit(solution)/shard_map/ppermute | solution.py:28
  133.6 6.2 %collective-permute-start.14 = (f32[1,1,128,128]{2,1,3,0:T(1,128)S(1)}, f32[1,1,128,128]{2,1,3,0:T(1,128)S(1)}, u32[]{:S(2)}, u32[]{:S(2)}) collective-permute-start(f32[1,1,128,128]{2,1,3,0:T(1,128)S(1)} %get-tuple-element.18), channel_id=1, source_target_pairs={{1,0},{2,1},{3,2},{4,3},{5,4},{6,5},{7,6},{8,7},{9,8},{10,9},{11,1... | collective-permute-start | bytes 196616 | tf_op jit(solution)/shard_map/ppermute | solution.py:29
  175.4 9.5 %collective-permute-start.16 = (f32[1,2,256]{2,1,0:T(2,128)S(1)}, f32[1,2,256]{2,1,0:T(2,128)S(1)}, u32[]{:S(2)}, u32[]{:S(2)}) collective-permute-start(f32[1,2,256]{2,1,0:T(2,128)S(1)} %bitcast.110), channel_id=1, source_target_pairs={{16,0},{32,16},{48,32},{64,48},{80,64},{96,80},{112,96},{128,112},... | collective-permute-start | bytes 6152 | tf_op jit(solution)/shard_map/ppermute | solution.py:29
  182.1 7.0 %collective-permute-start.15 = (f32[1,2,256]{2,1,0:T(2,128)S(1)}, f32[1,2,256]{2,1,0:T(2,128)S(1)}, u32[]{:S(2)}, u32[]{:S(2)}) collective-permute-start(f32[1,2,256]{2,1,0:T(2,128)S(1)} %bitcast.111), channel_id=1, source_target_pairs={{0,16},{16,32},{32,48},{48,64},{64,80},{80,96},{96,112},{112,128},... | collective-permute-start | bytes 6152 | tf_op jit(solution)/shard_map/ppermute | solution.py:28
  (2 other events, 1.9 us)
where the time goes:
time: 190 us
  blocking collectives  80.8 us (43%)
  starting transfers between devices  57.1 us (30%)
  waiting for transfers between devices  34.7 us (18%)
  other arithmetic  7.1 us (4%)
  local copies, waits for them, and re-layouts  5.61 us (3%)
  matrix products  3.32 us (2%)
    all_to_all x2, blocking collectives, from_everyone(): return lax.all_to_all(copies, axis, split_axis=0, concat_axis=0, tiled=True)  80.8 us
    ppermute x8, starting transfers between devices, with_halo(): before = lax.ppermute(last, axis, up)  39.4 us
    ppermute x8, waiting for transfers between devices, with_halo(): after = lax.ppermute(leading, axis, down)  24.3 us
    ppermute x8, starting transfers between devices, with_halo(): after = lax.ppermute(leading, axis, down)  16.5 us
    ppermute x8, waiting for transfers between devices, with_halo(): before = lax.ppermute(last, axis, up)  9.32 us
    unnamed x23, local copies, waits for them, and re-layouts  4.42 us
    add x5, other arithmetic, relax_pass(): return centre + RELAX * (rhs_part - applied) / part_diag  4.2 us
  transfers between devices with their start and end apart: 17, of which 12 were waited for; matrix products, arithmetic and copies ran while one was open for 3% of the time, Pallas kernels for 0%

commit v1 on v0

v1 whole, which is shorter than its diff:
```python
import functools
import jax
import jax.numpy as jnp
from jax import lax
from jax.experimental import pallas as pl
from jax.experimental.pallas import tpu as pltpu
from jax.sharding import PartitionSpec as P

RELAX = 0.8
MORTAR_STEP = 0.05
MESH = pl.DeviceIdType.MESH
GROUP = 4
CHUNKS = 4
F32 = jnp.float32


def roll(value, shift, axis):
    return pltpu.roll(value, shift % value.shape[axis], axis)


def kernel(
    sub_count, block_count,
    src_h, tx_h, ty_h, tz_h, mb_h, mt_h, p_out, m_out,
    src, tx, ty, tz, mb, mt,
    ayd, ayu, azd, azu, axd, axu, axh, face, wface, bias, press, pre, grid_g,
    d3, e1a, e1b, halo, cbuf, xr, zs, zr,
    load_sem, out_sem, e1_send, e1_recv, h_send, h_recv, x_send, x_recv, z_send, z_recv,
):
    layers, ny, nz = src.shape
    top = layers - 1
    mort = mb.shape[2]
    rows_m = mort // 128
    sub = lax.axis_index("sub")
    blk = lax.axis_index("block")
    xi = sub % GROUP
    zi = sub // GROUP
    zgroups = sub_count // GROUP
    has_low = sub > 0
    has_up = sub < sub_count - 1
    has_prev = blk > 0
    has_next = blk < block_count - 1
    rows_c = ny // CHUNKS

    loads = []
    for i, (h, v) in enumerate(((tx_h, tx), (ty_h, ty), (tz_h, tz), (src_h, src), (mb_h, mb), (mt_h, mt))):
        cp = pltpu.make_async_copy(h.at[0], v, load_sem.at[i])
        cp.start()
        loads.append(cp)

    barrier = pltpu.get_barrier_semaphore()

    def greet(b, s):
        pl.semaphore_signal(barrier, inc=1, device_id={"block": b, "sub": s}, device_id_type=MESH)

    def xpeer(j):
        return zi * GROUP + (xi + j) % GROUP

    slow_low = (xi == 0) & has_low
    slow_up = (xi == GROUP - 1) & has_up

    @pl.when(slow_low)
    def _():
        greet(blk, sub - 1)

    @pl.when(slow_up)
    def _():
        greet(blk, sub + 1)

    for j in range(1, GROUP):
        greet(blk, xpeer(j))
    for j in range(1, zgroups):
        greet(blk, (zi + j) % zgroups * GROUP + xi)

    @pl.when(has_prev)
    def _():
        for j in range(GROUP):
            greet(blk - 1, xpeer(j))

    @pl.when(has_next)
    def _():
        for j in range(GROUP):
            greet(blk + 1, xpeer(j))

    greeted = (
        GROUP - 1 + zgroups - 1
        + slow_low.astype(jnp.int32) + slow_up.astype(jnp.int32)
        + GROUP * has_prev.astype(jnp.int32) + GROUP * has_next.astype(jnp.int32)
    )

    zero_layer = jnp.zeros((ny, nz), F32)

    @pl.when(jnp.logical_not(has_low))
    def _():
        e1a[0] = zero_layer
        e1b[0] = zero_layer + 1.0
        for e in range(4):
            halo[e, 0] = zero_layer

    @pl.when(jnp.logical_not(has_up))
    def _():
        e1a[1] = zero_layer
        e1b[1] = zero_layer
        for e in range(4):
            halo[e, 1] = zero_layer

    zero_tile = jnp.zeros((8, 128), F32)
    for r in range(2):
        cbuf[r] = zero_tile
        zs[r] = zero_tile

    @pl.when(jnp.logical_not(has_next))
    def _():
        for r in range(2):
            for j in range(GROUP):
                xr[r, GROUP - 1 + j] = zero_tile

    @pl.when(jnp.logical_not(has_prev))
    def _():
        for r in range(2):
            for j in range(GROUP):
                xr[r, 2 * GROUP - 1 + j] = zero_tile

    iy = lax.broadcasted_iota(jnp.int32, (ny, nz), 0)
    iz = lax.broadcasted_iota(jnp.int32, (ny, nz), 1)
    bottom_cell = iz == 0
    top_cell = iz == nz - 1
    low_mask = has_low.astype(F32)
    prev_mask = has_prev.astype(F32)
    next_mask = has_next.astype(F32)

    loads[0].wait()
    loads[1].wait()
    loads[2].wait()
    loads[3].wait()

    def x_face(l):
        return tx[0] * low_mask if l == 0 else tx[l]

    def raw(l):
        cy = jnp.where(iy > 0, ty[l], 0.0)
        tzl = tz[l]
        cz = jnp.where(bottom_cell, 0.0, tzl)
        dirichlet = jnp.where(bottom_cell, tzl * prev_mask, 0.0) + jnp.where(top_cell, tzl * next_mask, 0.0)
        cyu = roll(cy, -1, 0)
        czu = roll(cz, -1, 1)
        return cy, cyu, cz, czu, dirichlet

    def keep(l, w, parts, low, up):
        cy, cyu, cz, czu, dirichlet = parts
        ayd[l] = w * cy
        ayu[l] = w * cyu
        azd[l] = w * cz
        azu[l] = w * czu
        wface[l] = w * dirichlet
        if l == 0:
            axh[0] = w * low
        else:
            axd[l] = w * low
        if l == top:
            axh[1] = w * up
        else:
            axu[l] = w * up
        b = w * src[l]
        bias[l] = b
        press[0, l] = b

    parts3 = raw(top)
    face[top] = parts3[4]
    d3[...] = x_face(top) + parts3[0] + parts3[1] + parts3[2] + parts3[3] + parts3[4]
    for l in range(top):
        parts = raw(l)
        face[l] = parts[4]
        low, up = x_face(l), tx[l + 1]
        diag = low + up + parts[0] + parts[1] + parts[2] + parts[3] + parts[4]
        keep(l, RELAX / diag, parts, low, up)

    pl.semaphore_wait(barrier, greeted)

    def e1_copy(i):
        source_ref, dest_ref, step = (
            (tx.at[0], e1a.at[1], -1),
            (press.at[0, 0], e1b.at[1], -1),
            (d3, e1b.at[0], 1),
            (src.at[top], e1a.at[0], 1),
        )[i]
        return pltpu.make_async_remote_copy(
            src_ref=source_ref, dst_ref=dest_ref, send_sem=e1_send.at[i], recv_sem=e1_recv.at[i],
            device_id={"block": blk, "sub": sub + step}, device_id_type=MESH,
        )

    @pl.when(has_low)
    def _():
        e1_copy(0).start()
        e1_copy(1).start()

    @pl.when(has_up)
    def _():
        e1_copy(2).start()
        e1_copy(3).start()

    def own_terms(k, l):
        p = press[k, l]
        return (
            (1.0 - RELAX) * p + bias[l]
            + ayd[l] * roll(p, 1, 0) + ayu[l] * roll(p, -1, 0)
            + azd[l] * roll(p, 1, 1) + azu[l] * roll(p, -1, 1)
        )

    def inner_layer(k, l):
        press[k + 1, l] = own_terms(k, l) + axd[l] * press[k, l - 1] + axu[l] * press[k, l + 1]

    def edge_terms(k, side):
        if side == 0:
            pre[0] = own_terms(k, 0) + axu[0] * press[k, 1]
        else:
            pre[1] = own_terms(k, top) + axd[top] * press[k, top - 1]

    def halo_copy(k, side, c):
        rows = pl.ds(c * rows_c, rows_c)
        return pltpu.make_async_remote_copy(
            src_ref=press.at[k, top * side, rows], dst_ref=halo.at[k - 1, 1 - side, rows],
            send_sem=h_send.at[k - 1, side, c], recv_sem=h_recv.at[k - 1, 1 - side, c],
            device_id={"block": blk, "sub": sub - 1 + 2 * side}, device_id_type=MESH,
        )

    def has(side):
        return jnp.where(side == 0, has_low.astype(jnp.int32), has_up.astype(jnp.int32)) > 0

    def send_side(k, side):
        @pl.when(has(side))
        def _():
            for c in range(CHUNKS):
                halo_copy(k, side, c).start()

    first_side = (xi != GROUP - 1).astype(jnp.int32)

    def edges(k, send):
        for t in range(2):
            side = first_side if t == 0 else 1 - first_side
            for c in range(CHUNKS):
                rows = pl.ds(c * rows_c, rows_c)

                @pl.when(has(side))
                def _():
                    halo_copy(k, 1 - side, c).wait_recv()

                press[k + 1, top * side, rows] = pre[side, rows] + axh[side, rows] * halo[k - 1, side, rows]
                if send:

                    @pl.when(has(side))
                    def _():
                        halo_copy(k + 1, side, c).start()

    inner_layer(0, 1)
    edge_terms(0, 0)

    @pl.when(has_up)
    def _():
        e1_copy(0).wait_recv()

    x_up = e1a[1]
    keep(top, RELAX / (d3[...] + x_up), raw(top), x_face(top), x_up)
    edge_terms(0, 1)

    @pl.when(has_up)
    def _():
        e1_copy(1).wait_recv()

    press[1, top] = pre[1] + axh[1] * e1b[1]
    send_side(1, 1)
    inner_layer(0, top - 1)

    @pl.when(has_low)
    def _():
        e1_copy(2).wait_recv()
        e1_copy(3).wait_recv()

    press[1, 0] = pre[0] + axh[0] * (RELAX * e1a[0] / (e1b[0] + x_face(0)))
    send_side(1, 0)

    def one_pass(k, send):
        for l in range(1, top):
            inner_layer(k, l)
        edge_terms(k, 0)
        edge_terms(k, 1)
        edges(k, send)

    one_pass(1, True)

    def project(k, with_g):
        acc_b = jnp.zeros((8, mort), F32)
        acc_t = jnp.zeros((8, mort), F32)
        for l in range(layers):
            p = press[k, l]
            f = face[l] * ((p - grid_g[l]) if with_g else p)
            fb = f[:, 0:1]
            ft = f[:, nz - 1 : nz]
            acc_b = acc_b + jnp.sum((fb * mb[l]).reshape(ny // 8, 8, mort), axis=0)
            acc_t = acc_t + jnp.sum((ft * mt[l]).reshape(ny // 8, 8, mort), axis=0)
        return jnp.sum(acc_t, axis=0, keepdims=True), jnp.sum(acc_b, axis=0, keepdims=True)

    def x_copy(r, i):
        if i < GROUP - 1:
            target = {"block": blk, "sub": xpeer(i + 1)}
        elif i < 2 * GROUP - 1:
            target = {"block": blk - 1, "sub": xpeer(i - GROUP + 1)}
        else:
            target = {"block": blk + 1, "sub": xpeer(i - 2 * GROUP + 1)}
        return pltpu.make_async_remote_copy(
            src_ref=cbuf.at[r], dst_ref=xr.at[r, i], send_sem=x_send.at[r, i], recv_sem=x_recv.at[r, i],
            device_id=target, device_id_type=MESH,
        )

    own = range(GROUP - 1)
    low_block = range(GROUP - 1, 2 * GROUP - 1)
    up_block = range(2 * GROUP - 1, 3 * GROUP - 1)

    def x_start(r, c_top, c_bot):
        for i in range(rows_m):
            cbuf[r, i : i + 1, :] = c_top[:, 128 * i : 128 * i + 128]
            cbuf[r, rows_m + i : rows_m + i + 1, :] = c_bot[:, 128 * i : 128 * i + 128]

        @pl.when(has_prev)
        def _():
            for i in low_block:
                x_copy(r, i).start()

        @pl.when(has_next)
        def _():
            for i in up_block:
                x_copy(r, i).start()

        for i in own:
            x_copy(r, i).start()

    def x_finish(r):
        for i in own:
            x_copy(r, i).wait_recv()

        @pl.when(has_next)
        def _():
            for i in low_block:
                x_copy(r, i).wait_recv()

        @pl.when(has_prev)
        def _():
            for i in up_block:
                x_copy(r, i).wait_recv()

        mine = cbuf[r]
        for i in own:
            mine = mine + xr[r, i]
        above = xr[r, low_block[0]]
        for i in low_block[1:]:
            above = above + xr[r, i]
        below = xr[r, up_block[0]]
        for i in up_block[1:]:
            below = below + xr[r, i]
        zs[r, 0:rows_m, :] = mine[0:rows_m] + above[rows_m : 2 * rows_m]
        zs[r, rows_m : 2 * rows_m, :] = below[0:rows_m] + mine[rows_m : 2 * rows_m]

    def z_copy(r, j):
        return pltpu.make_async_remote_copy(
            src_ref=zs.at[r], dst_ref=zr.at[r, j - 1], send_sem=z_send.at[r, j - 1], recv_sem=z_recv.at[r, j - 1],
            device_id={"block": blk, "sub": (zi + j) % zgroups * GROUP + xi}, device_id_type=MESH,
        )

    def z_start(r):
        for j in range(1, zgroups):
            z_copy(r, j).start()

    def z_finish(r):
        total = zs[r]
        for j in range(1, zgroups):
            z_copy(r, j).wait_recv()
            total = total + zr[r, j - 1]
        return MORTAR_STEP * total

    loads[4].wait()
    loads[5].wait()
    c_top, c_bot = project(2, False)
    x_start(0, c_top, c_bot)
    for l in range(1, top):
        inner_layer(2, l)
    edge_terms(2, 0)
    edge_terms(2, 1)
    x_finish(0)
    z_start(0)
    edges(2, False)
    mortar = z_finish(0)
    here = jnp.concatenate([mortar[i : i + 1, :] for i in range(rows_m)], axis=1)
    under = jnp.concatenate([mortar[rows_m + i : rows_m + i + 1, :] for i in range(rows_m)], axis=1)

    for l in (0, top) + tuple(range(1, top)):
        gb = jnp.sum(mb[l] * under, axis=1, keepdims=True)
        gt = jnp.sum(mt[l] * here, axis=1, keepdims=True)
        g = jnp.where(iz < nz // 2, gb, gt)
        grid_g[l] = g
        gain = wface[l] * g
        press[3, l] = press[3, l] + gain
        bias[l] = bias[l] + gain
        if l == 0:
            send_side(3, 0)
        if l == top:
            send_side(3, 1)

    one_pass(3, True)
    one_pass(4, False)

    out_copy = pltpu.make_async_copy(press.at[5], p_out.at[0], out_sem)
    out_copy.start()
    c_top, c_bot = project(5, True)
    x_start(1, c_top, c_bot)
    x_finish(1)
    z_start(1)
    final = mortar + z_finish(1)
    share = mort // sub_count
    offset = sub * share
    row = final[0:1, :]
    for i in range(1, rows_m):
        row = jnp.where(offset // 128 == i, final[i : i + 1, :], row)
    wide = jnp.broadcast_to(row, (8, 128))
    m_out[...] = pltpu.roll(wide, (128 - offset % 128) % 128, 1)[0:1, 0:share]

    out_copy.wait()

    @pl.when(has_low)
    def _():
        e1_copy(0).wait_send()
        e1_copy(1).wait_send()
        for k in range(1, 5):
            for c in range(CHUNKS):
                halo_copy(k, 0, c).wait_send()

    @pl.when(has_up)
    def _():
        e1_copy(2).wait_send()
        e1_copy(3).wait_send()
        for k in range(1, 5):
            for c in range(CHUNKS):
                halo_copy(k, 1, c).wait_send()

    for r in range(2):
        for i in own:
            x_copy(r, i).wait_send()
        for j in range(1, zgroups):
            z_copy(r, j).wait_send()

    @pl.when(has_prev)
    def _():
        for r in range(2):
            for i in low_block:
                x_copy(r, i).wait_send()

    @pl.when(has_next)
    def _():
        for r in range(2):
            for i in up_block:
                x_copy(r, i).wait_send()


def shards(source, trans_x, trans_y, trans_z, mortar_bot, mortar_top):
    _, layers, ny, nz = source.shape
    mort = mortar_bot.shape[3]
    sub_count = lax.axis_size("sub")
    block_count = lax.axis_size("block")
    zgroups = sub_count // GROUP
    field = pltpu.VMEM((layers, ny, nz), F32)
    basis = pltpu.VMEM((layers, ny, mort), F32)
    pair = pltpu.VMEM((2, ny, nz), F32)
    dma = pltpu.SemaphoreType.DMA
    xmsgs = 3 * GROUP - 1
    hbm = pl.BlockSpec(memory_space=pl.ANY)
    return pl.pallas_call(
        functools.partial(kernel, sub_count, block_count),
        out_shape=(
            jax.ShapeDtypeStruct(source.shape, F32),
            jax.ShapeDtypeStruct((1, mort // sub_count), F32),
        ),
        in_specs=[hbm] * 6,
        out_specs=(hbm, pl.BlockSpec(memory_space=pltpu.VMEM)),
        scratch_shapes=[
            field, field, field, field, basis, basis,
            field, field, field, field, field, field, pair, field, field, field,
            pltpu.VMEM((6, layers, ny, nz), F32), pair, field,
            pltpu.VMEM((ny, nz), F32), pair, pair, pltpu.VMEM((4, 2, ny, nz), F32),
            pltpu.VMEM((2, 8, 128), F32), pltpu.VMEM((2, xmsgs, 8, 128), F32),
            pltpu.VMEM((2, 8, 128), F32), pltpu.VMEM((2, zgroups - 1, 8, 128), F32),
            dma((6,)), dma, dma((4,)), dma((4,)),
            dma((4, 2, CHUNKS)), dma((4, 2, CHUNKS)),
            dma((2, xmsgs)), dma((2, xmsgs)), dma((2, zgroups - 1)), dma((2, zgroups - 1)),
        ],
        compiler_params=pltpu.CompilerParams(collective_id=0, has_side_effects=True),
        name="mortar_darcy",
    )(source, trans_x, trans_y, trans_z, mortar_bot, mortar_top)


def solution(mesh):
    spec = P("block", "sub", None, None)
    return jax.shard_map(
        shards,
        mesh=mesh,
        in_specs=(spec,) * 6,
        out_specs=(spec, P("block", "sub")),
        check_vma=False,
    )
```

time: 190 us -> 87.9 us (0.46)
  the two profiles are of different devices: /device:TPU:64 before, /device:TPU:89 now
where the time goes in v1:
time: 87.9 us; the launch traced here: 87.7 us
  Pallas kernels  84.9 us (97%)
  local copies, waits for them, and re-layouts  2.19 us (2%)
    pallas_call x1, Pallas kernels, shards(): pl.pallas_call(functools.partial(kernel, sub_count, block_count), out_sha...  84.9 us
    unnamed x4, local copies, waits for them, and re-layouts  2.19 us

profile of v1, /device:TPU:89, one launch (start us, length us, event | category | flops | bytes accessed | tf_op | source)
XLA Modules:
  0.0 87.7 jit_solution(1136355733641212870)
XLA Ops:
  0.6 84.9 %mortar_darcy.1 = (f32[1,4,128,128]{3,2,1,0:T(8,128)}, f32[1,16]{1,0:T(1,128)}) custom-call(f32[1,4,128,128]{3,2,1,0:T(8,128)} %src_h.1, f32[1,4,128,128]{3,2,1,0:T(8,128)} %tx_h.1, f32[1,4,128,128]{3,2,1,0:T(8,128)} %ty_h.1, f32[1,4,128,128]{3,2,1,0:T(8,128)} %tz_h.1, f32[1,4,128,256]{3,2,1,0:T(8,128)} %mb_h.1, f32[1,4,128,256]{3,2,1,0:T(8,128)} %mt_h.1), custom_call_target="tpu_custom_call" | custom-call | tf_op jit(solution)/shard_map/mortar_darcy/pallas_call | solution.py:474
  85.5 0.0 copy-start
  85.5 1.7 %copy.10 = f32[1,4,128,128]{3,2,1,0:T(8,128)} copy(f32[1,4,128,128]{3,2,1,0:T(8,128)} %get-tuple-element.4) | data formatting | bytes 524288
  87.2 0.0 copy-done
  87.2 0.5 copy.11
Async XLA Ops:
  85.5 1.7 %copy-start = (f32[1,16]{1,0:T(1,128)S(1)}, f32[1,16]{1,0:T(1,128)}, u32[]{:S(2)}) copy-start(f32[1,16]{1,0:T(1,128)} %get-tuple-element.5) | copy-start | bytes 196

commit v2 on v1

--- a/solution.py
+++ b/solution.py
@@ -11,6 +11,7 @@
 MESH = pl.DeviceIdType.MESH
 GROUP = 4
 CHUNKS = 4
+RELAYED = {1: 3, 2: 0, 3: 3, 4: 0}
 F32 = jnp.float32
 
 
@@ -22,9 +23,10 @@
     sub_count, block_count,
     src_h, tx_h, ty_h, tz_h, mb_h, mt_h, p_out, m_out,
     src, tx, ty, tz, mb, mt,
-    ayd, ayu, azd, azu, axd, axu, axh, face, wface, bias, press, pre, grid_g,
-    d3, e1a, e1b, halo, cbuf, xr, zs, zr,
-    load_sem, out_sem, e1_send, e1_recv, h_send, h_recv, x_send, x_recv, z_send, z_recv,
+    ayd, ayu, azd, azu, axd, axu, axh, face, wface, bias, press, pre, grid_g, grid_d,
+    d3, e1a, e1b, halo, cbuf, xr, zs, zr, part1, part, thin, thin_low, thin_up, g_own, g_halo,
+    load_sem, e1_send, e1_recv, h_send, h_recv, x_send, x_recv, z_send, z_recv,
+    p1_recv, f1_send, p_recv, f_send, t_send, t_recv, g_send, g_recv,
 ):
     layers, ny, nz = src.shape
     top = layers - 1
@@ -40,6 +42,12 @@
     has_prev = blk > 0
     has_next = blk < block_count - 1
     rows_c = ny // CHUNKS
+    rows_q = ny // GROUP
+    first_x = xi == 0
+    last_x = xi == GROUP - 1
+    group_low = zi > 0
+    group_up = zi < zgroups - 1
+    inside_x = jnp.logical_not(first_x | last_x)
 
     loads = []
     for i, (h, v) in enumerate(((tx_h, tx), (ty_h, ty), (tz_h, tz), (src_h, src), (mb_h, mb), (mt_h, mt))):
@@ -55,16 +63,28 @@
     def xpeer(j):
         return zi * GROUP + (xi + j) % GROUP
 
-    slow_low = (xi == 0) & has_low
-    slow_up = (xi == GROUP - 1) & has_up
+    slow_low = first_x & group_low
+    slow_up = last_x & group_up
+    pass_low = inside_x & group_low
+    pass_up = inside_x & group_up
 
     @pl.when(slow_low)
     def _():
-        greet(blk, sub - 1)
+        for j in range(1, GROUP):
+            greet(blk, sub - j)
 
     @pl.when(slow_up)
     def _():
-        greet(blk, sub + 1)
+        for j in range(1, GROUP):
+            greet(blk, sub + j)
+
+    @pl.when(pass_low)
+    def _():
+        greet(blk, (zi - 1) * GROUP + GROUP - 1)
+
+    @pl.when(pass_up)
+    def _():
+        greet(blk, (zi + 1) * GROUP)
 
     for j in range(1, GROUP):
         greet(blk, xpeer(j))
@@ -83,11 +103,13 @@
 
     greeted = (
         GROUP - 1 + zgroups - 1
-        + slow_low.astype(jnp.int32) + slow_up.astype(jnp.int32)
+        + (GROUP - 1) * (slow_low.astype(jnp.int32) + slow_up.astype(jnp.int32))
+        + pass_low.astype(jnp.int32) + pass_up.astype(jnp.int32)
         + GROUP * has_prev.astype(jnp.int32) + GROUP * has_next.astype(jnp.int32)
     )
 
     zero_layer = jnp.zeros((ny, nz), F32)
+    zero_thin = jnp.zeros((8, ny), F32)
 
     @pl.when(jnp.logical_not(has_low))
     def _():
@@ -95,6 +117,10 @@
         e1b[0] = zero_layer + 1.0
         for e in range(4):
             halo[e, 0] = zero_layer
+        g_halo[0] = zero_thin
+        for i in range(2):
+            for f in range(3):
+                thin_low[i, f] = zero_thin + 1.0
 
     @pl.when(jnp.logical_not(has_up))
     def _():
@@ -102,6 +128,10 @@
         e1b[1] = zero_layer
         for e in range(4):
             halo[e, 1] = zero_layer
+        g_halo[1] = zero_thin
+        for i in range(3):
+            for f in range(3):
+                thin_up[i, f] = zero_thin + (0.0 if i == 0 and f == 0 else 1.0)
 
     zero_tile = jnp.zeros((8, 128), F32)
     for r in range(2):
@@ -176,27 +206,76 @@
 
     pl.semaphore_wait(barrier, greeted)
 
-    def e1_copy(i):
+    def e1_copy(i, rows=None):
         source_ref, dest_ref, step = (
             (tx.at[0], e1a.at[1], -1),
             (press.at[0, 0], e1b.at[1], -1),
             (d3, e1b.at[0], 1),
             (src.at[top], e1a.at[0], 1),
         )[i]
+        if rows is not None:
+            source_ref, dest_ref = source_ref.at[rows], dest_ref.at[rows]
         return pltpu.make_async_remote_copy(
             src_ref=source_ref, dst_ref=dest_ref, send_sem=e1_send.at[i], recv_sem=e1_recv.at[i],
             device_id={"block": blk, "sub": sub + step}, device_id_type=MESH,
         )
 
-    @pl.when(has_low)
-    def _():
-        e1_copy(0).start()
-        e1_copy(1).start()
-
-    @pl.when(has_up)
-    def _():
-        e1_copy(2).start()
-        e1_copy(3).start()
+    def e1_part(i, c):
+        source_ref = (tx.at[0], press.at[0, 0], d3, src.at[top])[i]
+        helper = (xi + c) % GROUP if i >= 2 else (xi + GROUP - c) % GROUP
+        return pltpu.make_async_remote_copy(
+            src_ref=source_ref.at[pl.ds(c * rows_q, rows_q)], dst_ref=part1.at[i],
+            send_sem=e1_send.at[i], recv_sem=p1_recv.at[i],
+            device_id={"block": blk, "sub": zi * GROUP + helper}, device_id_type=MESH,
+        )
+
+    def e1_forward(i):
+        dest_ref = (e1a.at[1], e1b.at[1], e1b.at[0], e1a.at[0])[i]
+        if i >= 2:
+            c, target = (xi + 1) % GROUP, (zi + 1) * GROUP
+        else:
+            c, target = (GROUP - xi) % GROUP, (zi - 1) * GROUP + GROUP - 1
+        return pltpu.make_async_remote_copy(
+            src_ref=part1.at[i], dst_ref=dest_ref.at[pl.ds(c * rows_q, rows_q)],
+            send_sem=f1_send.at[i], recv_sem=e1_recv.at[i],
+            device_id={"block": blk, "sub": target}, device_id_type=MESH,
+        )
+
+    helps_low = jnp.logical_not(first_x) & group_low
+    helps_up = jnp.logical_not(last_x) & group_up
+
+    for across, pair in ((slow_low, (0, 1)), (slow_up, (2, 3))):
+
+        @pl.when(across)
+        def _():
+            for c in (2, 1, 3):
+                for i in pair:
+                    e1_part(i, c).start()
+            for i in pair:
+                e1_copy(i, pl.ds(0, rows_q)).start()
+
+    for beside, pair in ((jnp.logical_not(first_x), (0, 1)), (jnp.logical_not(last_x), (2, 3))):
+
+        @pl.when(beside)
+        def _():
+            for i in pair:
+                e1_copy(i).start()
+
+    thin_row = lax.broadcasted_iota(jnp.int32, (8, ny), 0)
+    thin_y = lax.broadcasted_iota(jnp.int32, (8, ny), 1)
+    for l in range(layers):
+        for f, ref in enumerate((tx, ty, tz)):
+            turned = ref[l].T
+            value = jnp.where(thin_row < 4, turned[0:8], turned[nz - 8 : nz])
+            thin[l, f] = value * low_mask if l == 0 and f == 0 else value
+
+    for helps, pair in ((helps_low, (0, 1)), (helps_up, (2, 3))):
+
+        @pl.when(helps)
+        def _():
+            for i in pair:
+                e1_part(i, 1).wait_recv()
+                e1_forward(i).start()
 
     def own_terms(k, l):
         p = press[k, l]
@@ -223,21 +302,67 @@
             device_id={"block": blk, "sub": sub - 1 + 2 * side}, device_id_type=MESH,
         )
 
+    def part_copy(k, side):
+        return pltpu.make_async_remote_copy(
+            src_ref=press.at[k, top * side, pl.ds(RELAYED[k] * rows_c, rows_c)], dst_ref=part.at[k - 1],
+            send_sem=h_send.at[k - 1, side, RELAYED[k]], recv_sem=p_recv.at[k - 1],
+            device_id={"block": blk, "sub": sub + 1 - 2 * side}, device_id_type=MESH,
+        )
+
+    help_side = (xi == GROUP - 2).astype(jnp.int32)
+    helps = ((xi == GROUP - 2) & group_up) | ((xi == 1) & group_low)
+
+    def forward_copy(k):
+        return pltpu.make_async_remote_copy(
+            src_ref=part.at[k - 1],
+            dst_ref=halo.at[k - 1, 1 - help_side, pl.ds(RELAYED[k] * rows_c, rows_c)],
+            send_sem=f_send.at[k - 1], recv_sem=h_recv.at[k - 1, 1 - help_side, RELAYED[k]],
+            device_id={"block": blk, "sub": (zi - 1 + 2 * help_side) * GROUP + (1 - help_side) * (GROUP - 1)},
+            device_id_type=MESH,
+        )
+
+    def forward(k):
+        if RELAYED[k] is None:
+            return
+
+        @pl.when(helps)
+        def _():
+            part_copy(k, help_side).wait_recv()
+            forward_copy(k).start()
+
     def has(side):
         return jnp.where(side == 0, has_low.astype(jnp.int32), has_up.astype(jnp.int32)) > 0
 
+    def slow(side):
+        return jnp.where(side == 0, first_x.astype(jnp.int32), last_x.astype(jnp.int32)) > 0
+
+    def send_chunk(k, side, c):
+        if c != RELAYED[k]:
+
+            @pl.when(has(side))
+            def _():
+                halo_copy(k, side, c).start()
+
+        else:
+
+            @pl.when(has(side) & jnp.logical_not(slow(side)))
+            def _():
+                halo_copy(k, side, c).start()
+
+            @pl.when(has(side) & slow(side))
+            def _():
+                part_copy(k, side).start()
+
     def send_side(k, side):
-        @pl.when(has(side))
-        def _():
-            for c in range(CHUNKS):
-                halo_copy(k, side, c).start()
-
-    first_side = (xi != GROUP - 1).astype(jnp.int32)
+        for c in sorted(range(CHUNKS), key=lambda c: c != RELAYED[k]):
+            send_chunk(k, side, c)
+
+    first_side = jnp.logical_not(last_x).astype(jnp.int32)
 
     def edges(k, send):
         for t in range(2):
             side = first_side if t == 0 else 1 - first_side
-            for c in range(CHUNKS):
+            for c in sorted(range(CHUNKS), key=lambda c: c == RELAYED[k]):
                 rows = pl.ds(c * rows_c, rows_c)
 
                 @pl.when(has(side))
@@ -246,13 +371,23 @@
 
                 press[k + 1, top * side, rows] = pre[side, rows] + axh[side, rows] * halo[k - 1, side, rows]
                 if send:
-
-                    @pl.when(has(side))
-                    def _():
-                        halo_copy(k + 1, side, c).start()
+                    send_chunk(k + 1, side, c)
 
     inner_layer(0, 1)
     edge_terms(0, 0)
+
+    def low_edge():
+        @pl.when(has_low)
+        def _():
+            e1_copy(2).wait_recv()
+            e1_copy(3).wait_recv()
+
+        press[1, 0] = pre[0] + axh[0] * (RELAX * e1a[0] / (e1b[0] + x_face(0)))
+        send_side(1, 0)
+
+    @pl.when(last_x)
+    def _():
+        low_edge()
 
     @pl.when(has_up)
     def _():
@@ -270,13 +405,9 @@
     send_side(1, 1)
     inner_layer(0, top - 1)
 
-    @pl.when(has_low)
-    def _():
-        e1_copy(2).wait_recv()
-        e1_copy(3).wait_recv()
-
-    press[1, 0] = pre[0] + axh[0] * (RELAX * e1a[0] / (e1b[0] + x_face(0)))
-    send_side(1, 0)
+    @pl.when(jnp.logical_not(last_x))
+    def _():
+        low_edge()
 
     def one_pass(k, send):
         for l in range(1, top):
@@ -286,18 +417,45 @@
         edges(k, send)
 
     one_pass(1, True)
-
-    def project(k, with_g):
-        acc_b = jnp.zeros((8, mort), F32)
-        acc_t = jnp.zeros((8, mort), F32)
-        for l in range(layers):
-            p = press[k, l]
+    forward(1)
+
+    def thin_copy(side):
+        low = side == 0
+        return pltpu.make_async_remote_copy(
+            src_ref=thin.at[0:3] if low else thin.at[layers - 2 : layers],
+            dst_ref=thin_up if low else thin_low,
+            send_sem=t_send.at[side], recv_sem=t_recv.at[1 - side],
+            device_id={"block": blk, "sub": sub - 1 + 2 * side}, device_id_type=MESH,
+        )
+
+    def g_copy(side):
+        return pltpu.make_async_remote_copy(
+            src_ref=g_own, dst_ref=g_halo.at[1 - side], send_sem=g_send.at[side], recv_sem=g_recv.at[1 - side],
+            device_id={"block": blk, "sub": sub - 1 + 2 * side}, device_id_type=MESH,
+        )
+
+    def on_sides(act):
+        @pl.when(has_low)
+        def _():
+            act(0)
+
+        @pl.when(has_up)
+        def _():
+            act(1)
+
+    on_sides(lambda side: thin_copy(side).start())
+
+    def project(acc, values, with_g):
+        acc_t, acc_b = acc
+        for l, p in values:
             f = face[l] * ((p - grid_g[l]) if with_g else p)
             fb = f[:, 0:1]
             ft = f[:, nz - 1 : nz]
             acc_b = acc_b + jnp.sum((fb * mb[l]).reshape(ny // 8, 8, mort), axis=0)
             acc_t = acc_t + jnp.sum((ft * mt[l]).reshape(ny // 8, 8, mort), axis=0)
-        return jnp.sum(acc_t, axis=0, keepdims=True), jnp.sum(acc_b, axis=0, keepdims=True)
+        return acc_t, acc_b
+
+    no_flux = (jnp.zeros((8, mort), F32), jnp.zeros((8, mort), F32))
 
     def x_copy(r, i):
         if i < GROUP - 1:
@@ -315,7 +473,8 @@
     low_block = range(GROUP - 1, 2 * GROUP - 1)
     up_block = range(2 * GROUP - 1, 3 * GROUP - 1)
 
-    def x_start(r, c_top, c_bot):
+    def x_start(r, acc):
+        c_top, c_bot = (jnp.sum(v, axis=0, keepdims=True) for v in acc)
         for i in range(rows_m):
             cbuf[r, i : i + 1, :] = c_top[:, 128 * i : 128 * i + 128]
             cbuf[r, rows_m + i : rows_m + i + 1, :] = c_bot[:, 128 * i : 128 * i + 128]
@@ -378,39 +537,93 @@
 
     loads[4].wait()
     loads[5].wait()
-    c_top, c_bot = project(2, False)
-    x_start(0, c_top, c_bot)
+    x_start(0, project(no_flux, [(l, press[2, l]) for l in range(layers)], False))
     for l in range(1, top):
         inner_layer(2, l)
     edge_terms(2, 0)
     edge_terms(2, 1)
+    forward(2)
     x_finish(0)
     z_start(0)
-    edges(2, False)
+    edges(2, True)
+    forward(3)
     mortar = z_finish(0)
     here = jnp.concatenate([mortar[i : i + 1, :] for i in range(rows_m)], axis=1)
     under = jnp.concatenate([mortar[rows_m + i : rows_m + i + 1, :] for i in range(rows_m)], axis=1)
 
+    columns = zero_layer
     for l in (0, top) + tuple(range(1, top)):
         gb = jnp.sum(mb[l] * under, axis=1, keepdims=True)
         gt = jnp.sum(mt[l] * here, axis=1, keepdims=True)
-        g = jnp.where(iz < nz // 2, gb, gt)
-        grid_g[l] = g
-        gain = wface[l] * g
-        press[3, l] = press[3, l] + gain
-        bias[l] = bias[l] + gain
-        if l == 0:
-            send_side(3, 0)
-        if l == top:
-            send_side(3, 1)
+        columns = jnp.where(iz == l, gb, columns)
+        columns = jnp.where(iz == layers + l, gt, columns)
+        grid_g[l] = jnp.where(iz < nz // 2, gb, gt)
+    g_own[...] = columns.T[0 : 2 * layers]
+    on_sides(lambda side: g_copy(side).start())
 
     one_pass(3, True)
-    one_pass(4, False)
-
-    out_copy = pltpu.make_async_copy(press.at[5], p_out.at[0], out_sem)
-    out_copy.start()
-    c_top, c_bot = project(5, True)
-    x_start(1, c_top, c_bot)
+    forward(4)
+    for l in range(1, top):
+        inner_layer(4, l)
+    edge_terms(4, 0)
+    edge_terms(4, 1)
+
+    on_sides(lambda side: thin_copy(1 - side).wait_recv())
+    on_sides(lambda side: g_copy(1 - side).wait_recv())
+
+    def thin_at(j, f):
+        if j < 0:
+            return thin_low[j + 2, f]
+        return thin[j, f] if j < layers else thin_up[j - layers, f]
+
+    def g_at(j):
+        i = j % layers
+        ref = g_halo.at[0] if j < 0 else g_own if j < layers else g_halo.at[1]
+        return jnp.where(thin_row < 4, ref[i : i + 1, :], ref[layers + i : layers + i + 1, :])
+
+    def thin_terms(j):
+        low, up = thin_at(j, 0), thin_at(j + 1, 0)
+        cy = jnp.where(thin_y > 0, thin_at(j, 1), 0.0)
+        tzj = thin_at(j, 2)
+        cz = jnp.where(thin_row > 0, tzj, 0.0)
+        cyu = roll(cy, -1, 1)
+        czu = roll(cz, -1, 0)
+        dirichlet = jnp.where(thin_row == 0, tzj * prev_mask, 0.0) + jnp.where(thin_row == 7, tzj * next_mask, 0.0)
+        w = RELAX / (low + up + cy + cyu + cz + czu + dirichlet)
+        return w, low, up, cy, cyu, cz, czu, w * dirichlet * g_at(j)
+
+    terms = {j: thin_terms(j) for j in range(-2, layers + 2)}
+
+    def thin_pass(v, j):
+        w, low, up, cy, cyu, cz, czu, b = terms[j]
+        d = v[j]
+        return (1.0 - RELAX) * d + b + w * (
+            low * v[j - 1] + up * v[j + 1]
+            + cy * roll(d, 1, 1) + cyu * roll(d, -1, 1) + cz * roll(d, 1, 0) + czu * roll(d, -1, 0)
+        )
+
+    first = {j: terms[j][7] for j in range(-2, layers + 2)}
+    second = {j: thin_pass(first, j) for j in range(-1, layers + 1)}
+    third = {j: thin_pass(second, j) for j in range(layers)}
+
+    def added(l):
+        d = third[l]
+        tall = jnp.concatenate(
+            [jnp.where(thin_row < 4, d, 0.0), jnp.zeros((nz - 16, ny), F32), jnp.where(thin_row < 4, 0.0, d)], axis=0
+        )
+        return tall.T
+
+    def finish_layer(l):
+        p = press[5, l] + grid_d[l]
+        p_out[0, l] = p
+        return l, p
+
+    for l in range(layers):
+        grid_d[l] = added(l)
+    flux = project(no_flux, [finish_layer(l) for l in range(1, top)], True)
+    edges(4, False)
+    flux = project(flux, [finish_layer(l) for l in (0, top)], True)
+    x_start(1, flux)
     x_finish(1)
     z_start(1)
     final = mortar + z_finish(1)
@@ -422,7 +635,8 @@
     wide = jnp.broadcast_to(row, (8, 128))
     m_out[...] = pltpu.roll(wide, (128 - offset % 128) % 128, 1)[0:1, 0:share]
 
-    out_copy.wait()
+    on_sides(lambda side: thin_copy(side).wait_send())
+    on_sides(lambda side: g_copy(side).wait_send())
 
     @pl.when(has_low)
     def _():
@@ -439,6 +653,22 @@
         for k in range(1, 5):
             for c in range(CHUNKS):
                 halo_copy(k, 1, c).wait_send()
+
+    @pl.when(helps_low)
+    def _():
+        e1_forward(0).wait_send()
+        e1_forward(1).wait_send()
+
+    @pl.when(helps_up)
+    def _():
+        e1_forward(2).wait_send()
+        e1_forward(3).wait_send()
+
+    @pl.when(helps)
+    def _():
+        for k in range(1, 5):
+            if RELAYED[k] is not None:
+                forward_copy(k).wait_send()
 
     for r in range(2):
         for i in own:
@@ -471,24 +701,30 @@
     dma = pltpu.SemaphoreType.DMA
     xmsgs = 3 * GROUP - 1
     hbm = pl.BlockSpec(memory_space=pl.ANY)
+    vmem = pl.BlockSpec(memory_space=pltpu.VMEM)
     return pl.pallas_call(
         functools.partial(kernel, sub_count, block_count),
         out_shape=(
-            jax.ShapeDtypeStruct(source.shape, F32),
-            jax.ShapeDtypeStruct((1, mort // sub_count), F32),
+            pltpu.VMEM(source.shape, F32),
+            pltpu.VMEM((1, mort // sub_count), F32),
         ),
         in_specs=[hbm] * 6,
-        out_specs=(hbm, pl.BlockSpec(memory_space=pltpu.VMEM)),
+        out_specs=(vmem, vmem),
         scratch_shapes=[
             field, field, field, field, basis, basis,
             field, field, field, field, field, field, pair, field, field, field,
-            pltpu.VMEM((6, layers, ny, nz), F32), pair, field,
+            pltpu.VMEM((6, layers, ny, nz), F32), pair, field, field,
             pltpu.VMEM((ny, nz), F32), pair, pair, pltpu.VMEM((4, 2, ny, nz), F32),
             pltpu.VMEM((2, 8, 128), F32), pltpu.VMEM((2, xmsgs, 8, 128), F32),
             pltpu.VMEM((2, 8, 128), F32), pltpu.VMEM((2, zgroups - 1, 8, 128), F32),
-            dma((6,)), dma, dma((4,)), dma((4,)),
+            pltpu.VMEM((4, ny // GROUP, nz), F32), pltpu.VMEM((4, ny // CHUNKS, nz), F32),
+            pltpu.VMEM((layers, 3, 8, ny), F32), pltpu.VMEM((2, 3, 8, ny), F32), pltpu.VMEM((3, 3, 8, ny), F32),
+            pltpu.VMEM((2 * layers, ny), F32), pltpu.VMEM((2, 2 * layers, ny), F32),
+            dma((6,)), dma((4,)), dma((4,)),
             dma((4, 2, CHUNKS)), dma((4, 2, CHUNKS)),
             dma((2, xmsgs)), dma((2, xmsgs)), dma((2, zgroups - 1)), dma((2, zgroups - 1)),
+            dma((4,)), dma((4,)), dma((4,)), dma((4,)),
+            dma((2,)), dma((2,)), dma((2,)), dma((2,)),
         ],
         compiler_params=pltpu.CompilerParams(collective_id=0, has_side_effects=True),
         name="mortar_darcy",

time: 87.9 us -> 76.8 us (0.87)
  the two profiles are of different devices: /device:TPU:89 before, /device:TPU:64 now
where the time goes in v2:
time: 76.8 us; the launch traced here: 76.6 us
  Pallas kernels  74.8 us (97%)
  local copies, waits for them, and re-layouts  1.22 us (2%)
    pallas_call x1, Pallas kernels, shards(): pl.pallas_call(functools.partial(kernel, sub_count, block_count), out_sha...  74.8 us

profile of v2, /device:TPU:64, one launch (start us, length us, event | category | flops | bytes accessed | tf_op | source)
XLA Modules:
  0.0 76.6 jit_solution(11224087134998882232)
XLA Ops:
  0.6 74.8 %mortar_darcy.1 = (f32[1,4,128,128]{3,2,1,0:T(8,128)S(1)}, f32[1,16]{1,0:T(1,128)S(1)}) custom-call(f32[1,4,128,128]{3,2,1,0:T(8,128)} %src_h.1, f32[1,4,128,128]{3,2,1,0:T(8,128)} %tx_h.1, f32[1,4,128,128]{3,2,1,0:T(8,128)} %ty_h.1, f32[1,4,128,128]{3,2,1,0:T(8,128)} %tz_h.1, f32[1,4,128,256]{3,2,1,0:T(8,128)} %mb_h.1, f32[1,4,128,256]{3,2,1,0:T(8,128)} %mt_h.1), custom_call_target="tpu_custom_call" | custom-call | tf_op jit(solution)/shard_map/mortar_darcy/pallas_call | solution.py:705
  75.4 0.7 copy.10
  76.1 0.5 copy.11

commit v3 on v2

--- a/solution.py
+++ b/solution.py
@@ -23,10 +23,10 @@
     sub_count, block_count,
     src_h, tx_h, ty_h, tz_h, mb_h, mt_h, p_out, m_out,
     src, tx, ty, tz, mb, mt,
-    ayd, ayu, azd, azu, axd, axu, axh, face, wface, bias, press, pre, grid_g, grid_d,
-    d3, e1a, e1b, halo, cbuf, xr, zs, zr, part1, part, thin, thin_low, thin_up, g_own, g_halo,
+    ayd, ayu, azd, azu, axd, axu, axh, bias, press, pre, grid_d,
+    d3, e1a, e1b, halo, cbuf, xr, zs, zr, part1, part, thin, thin_low, thin_up, near, near_low, near_up, g_own, g_halo,
     load_sem, e1_send, e1_recv, h_send, h_recv, x_send, x_recv, z_send, z_recv,
-    p1_recv, f1_send, p_recv, f_send, t_send, t_recv, g_send, g_recv,
+    p1_recv, f1_send, p_recv, f_send, t_send, t_recv, n_send, n_recv, g_send, g_recv,
 ):
     layers, ny, nz = src.shape
     top = layers - 1
@@ -119,8 +119,10 @@
             halo[e, 0] = zero_layer
         g_halo[0] = zero_thin
         for i in range(2):
-            for f in range(3):
-                thin_low[i, f] = zero_thin + 1.0
+            for f in range(4):
+                thin_low[i, f] = zero_thin + (0.0 if f == 3 else 1.0)
+        for i in range(3):
+            near_low[i] = zero_thin
 
     @pl.when(jnp.logical_not(has_up))
     def _():
@@ -130,8 +132,10 @@
             halo[e, 1] = zero_layer
         g_halo[1] = zero_thin
         for i in range(3):
-            for f in range(3):
-                thin_up[i, f] = zero_thin + (0.0 if i == 0 and f == 0 else 1.0)
+            for f in range(4):
+                thin_up[i, f] = zero_thin + (0.0 if f == 3 or (i == 0 and f == 0) else 1.0)
+        for i in range(3):
+            near_up[i] = zero_thin
 
     zero_tile = jnp.zeros((8, 128), F32)
     for r in range(2):
@@ -181,7 +185,6 @@
         ayu[l] = w * cyu
         azd[l] = w * cz
         azu[l] = w * czu
-        wface[l] = w * dirichlet
         if l == 0:
             axh[0] = w * low
         else:
@@ -195,16 +198,63 @@
         press[0, l] = b
 
     parts3 = raw(top)
-    face[top] = parts3[4]
     d3[...] = x_face(top) + parts3[0] + parts3[1] + parts3[2] + parts3[3] + parts3[4]
     for l in range(top):
         parts = raw(l)
-        face[l] = parts[4]
         low, up = x_face(l), tx[l + 1]
         diag = low + up + parts[0] + parts[1] + parts[2] + parts[3] + parts[4]
         keep(l, RELAX / diag, parts, low, up)
 
+    thin_row = lax.broadcasted_iota(jnp.int32, (8, ny), 0)
+    thin_y = lax.broadcasted_iota(jnp.int32, (8, ny), 1)
+
+    def thinned(layer):
+        turned = layer.T
+        return jnp.where(thin_row < 4, turned[0:8], turned[nz - 8 : nz])
+
+    for l in range(layers):
+        for f, ref in enumerate((tx, ty, tz, src)):
+            value = thinned(ref[l])
+            thin[l, f] = value * low_mask if l == 0 and f == 0 else value
+
     pl.semaphore_wait(barrier, greeted)
+
+    def on_sides(act):
+        @pl.when(has_low)
+        def _():
+            act(0)
+
+        @pl.when(has_up)
+        def _():
+            act(1)
+
+    def side_copy(side, source_ref, dest_ref, send_sem, recv_sem):
+        return pltpu.make_async_remote_copy(
+            src_ref=source_ref, dst_ref=dest_ref, send_sem=send_sem, recv_sem=recv_sem,
+            device_id={"block": blk, "sub": sub - 1 + 2 * side}, device_id_type=MESH,
+        )
+
+    def thin_copies(side):
+        if side == 0:
+            return (
+                side_copy(0, thin.at[0:2], thin_up.at[0:2], t_send.at[0], t_recv.at[0]),
+                side_copy(0, thin.at[2, 0], thin_up.at[2, 0], t_send.at[1], t_recv.at[1]),
+            )
+        return (side_copy(1, thin.at[layers - 2 : layers], thin_low, t_send.at[2], t_recv.at[2]),)
+
+    def near_copy(side):
+        if side == 0:
+            return side_copy(0, near.at[0:3], near_up, n_send.at[0], n_recv.at[0])
+        return side_copy(1, near.at[layers - 3 : layers], near_low, n_send.at[1], n_recv.at[1])
+
+    def g_copy(side):
+        return side_copy(side, g_own, g_halo.at[1 - side], g_send.at[side], g_recv.at[1 - side])
+
+    def start_all(copies):
+        for copy in copies:
+            copy.start()
+
+    on_sides(lambda side: start_all(thin_copies(side)))
 
     def e1_copy(i, rows=None):
         source_ref, dest_ref, step = (
@@ -261,14 +311,6 @@
             for i in pair:
                 e1_copy(i).start()
 
-    thin_row = lax.broadcasted_iota(jnp.int32, (8, ny), 0)
-    thin_y = lax.broadcasted_iota(jnp.int32, (8, ny), 1)
-    for l in range(layers):
-        for f, ref in enumerate((tx, ty, tz)):
-            turned = ref[l].T
-            value = jnp.where(thin_row < 4, turned[0:8], turned[nz - 8 : nz])
-            thin[l, f] = value * low_mask if l == 0 and f == 0 else value
-
     for helps, pair in ((helps_low, (0, 1)), (helps_up, (2, 3))):
 
         @pl.when(helps)
@@ -372,90 +414,6 @@
                 press[k + 1, top * side, rows] = pre[side, rows] + axh[side, rows] * halo[k - 1, side, rows]
                 if send:
                     send_chunk(k + 1, side, c)
-
-    inner_layer(0, 1)
-    edge_terms(0, 0)
-
-    def low_edge():
-        @pl.when(has_low)
-        def _():
-            e1_copy(2).wait_recv()
-            e1_copy(3).wait_recv()
-
-        press[1, 0] = pre[0] + axh[0] * (RELAX * e1a[0] / (e1b[0] + x_face(0)))
-        send_side(1, 0)
-
-    @pl.when(last_x)
-    def _():
-        low_edge()
-
-    @pl.when(has_up)
-    def _():
-        e1_copy(0).wait_recv()
-
-    x_up = e1a[1]
-    keep(top, RELAX / (d3[...] + x_up), raw(top), x_face(top), x_up)
-    edge_terms(0, 1)
-
-    @pl.when(has_up)
-    def _():
-        e1_copy(1).wait_recv()
-
-    press[1, top] = pre[1] + axh[1] * e1b[1]
-    send_side(1, 1)
-    inner_layer(0, top - 1)
-
-    @pl.when(jnp.logical_not(last_x))
-    def _():
-        low_edge()
-
-    def one_pass(k, send):
-        for l in range(1, top):
-            inner_layer(k, l)
-        edge_terms(k, 0)
-        edge_terms(k, 1)
-        edges(k, send)
-
-    one_pass(1, True)
-    forward(1)
-
-    def thin_copy(side):
-        low = side == 0
-        return pltpu.make_async_remote_copy(
-            src_ref=thin.at[0:3] if low else thin.at[layers - 2 : layers],
-            dst_ref=thin_up if low else thin_low,
-            send_sem=t_send.at[side], recv_sem=t_recv.at[1 - side],
-            device_id={"block": blk, "sub": sub - 1 + 2 * side}, device_id_type=MESH,
-        )
-
-    def g_copy(side):
-        return pltpu.make_async_remote_copy(
-            src_ref=g_own, dst_ref=g_halo.at[1 - side], send_sem=g_send.at[side], recv_sem=g_recv.at[1 - side],
-            device_id={"block": blk, "sub": sub - 1 + 2 * side}, device_id_type=MESH,
-        )
-
-    def on_sides(act):
-        @pl.when(has_low)
-        def _():
-            act(0)
-
-        @pl.when(has_up)
-        def _():
-            act(1)
-
-    on_sides(lambda side: thin_copy(side).start())
-
-    def project(acc, values, with_g):
-        acc_t, acc_b = acc
-        for l, p in values:
-            f = face[l] * ((p - grid_g[l]) if with_g else p)
-            fb = f[:, 0:1]
-            ft = f[:, nz - 1 : nz]
-            acc_b = acc_b + jnp.sum((fb * mb[l]).reshape(ny // 8, 8, mort), axis=0)
-            acc_t = acc_t + jnp.sum((ft * mt[l]).reshape(ny // 8, 8, mort), axis=0)
-        return acc_t, acc_b
-
-    no_flux = (jnp.zeros((8, mort), F32), jnp.zeros((8, mort), F32))
 
     def x_copy(r, i):
         if i < GROUP - 1:
@@ -535,51 +493,28 @@
             total = total + zr[r, j - 1]
         return MORTAR_STEP * total
 
-    loads[4].wait()
-    loads[5].wait()
-    x_start(0, project(no_flux, [(l, press[2, l]) for l in range(layers)], False))
-    for l in range(1, top):
-        inner_layer(2, l)
-    edge_terms(2, 0)
-    edge_terms(2, 1)
-    forward(2)
-    x_finish(0)
-    z_start(0)
-    edges(2, True)
-    forward(3)
-    mortar = z_finish(0)
-    here = jnp.concatenate([mortar[i : i + 1, :] for i in range(rows_m)], axis=1)
-    under = jnp.concatenate([mortar[rows_m + i : rows_m + i + 1, :] for i in range(rows_m)], axis=1)
-
-    columns = zero_layer
-    for l in (0, top) + tuple(range(1, top)):
-        gb = jnp.sum(mb[l] * under, axis=1, keepdims=True)
-        gt = jnp.sum(mt[l] * here, axis=1, keepdims=True)
-        columns = jnp.where(iz == l, gb, columns)
-        columns = jnp.where(iz == layers + l, gt, columns)
-        grid_g[l] = jnp.where(iz < nz // 2, gb, gt)
-    g_own[...] = columns.T[0 : 2 * layers]
-    on_sides(lambda side: g_copy(side).start())
-
-    one_pass(3, True)
-    forward(4)
-    for l in range(1, top):
-        inner_layer(4, l)
-    edge_terms(4, 0)
-    edge_terms(4, 1)
-
-    on_sides(lambda side: thin_copy(1 - side).wait_recv())
-    on_sides(lambda side: g_copy(1 - side).wait_recv())
+    def project(fluxes):
+        flat = jnp.concatenate([fluxes, jnp.zeros((128 - 2 * layers, ny), F32)], axis=0).T
+        acc_t = jnp.zeros((8, mort), F32)
+        acc_b = jnp.zeros((8, mort), F32)
+        for l in range(layers):
+            fb = flat[:, l : l + 1]
+            ft = flat[:, layers + l : layers + l + 1]
+            acc_b = acc_b + jnp.sum((fb * mb[l]).reshape(ny // 8, 8, mort), axis=0)
+            acc_t = acc_t + jnp.sum((ft * mt[l]).reshape(ny // 8, 8, mort), axis=0)
+        return acc_t, acc_b
+
+    def face_rows(tiles):
+        out = zero_thin
+        for l in range(layers):
+            out = jnp.where(thin_row == l, tiles[l][0:1, :], out)
+            out = jnp.where(thin_row == layers + l, tiles[l][7:8, :], out)
+        return out
 
     def thin_at(j, f):
         if j < 0:
             return thin_low[j + 2, f]
         return thin[j, f] if j < layers else thin_up[j - layers, f]
-
-    def g_at(j):
-        i = j % layers
-        ref = g_halo.at[0] if j < 0 else g_own if j < layers else g_halo.at[1]
-        return jnp.where(thin_row < 4, ref[i : i + 1, :], ref[layers + i : layers + i + 1, :])
 
     def thin_terms(j):
         low, up = thin_at(j, 0), thin_at(j + 1, 0)
@@ -590,42 +525,157 @@
         czu = roll(cz, -1, 0)
         dirichlet = jnp.where(thin_row == 0, tzj * prev_mask, 0.0) + jnp.where(thin_row == 7, tzj * next_mask, 0.0)
         w = RELAX / (low + up + cy + cyu + cz + czu + dirichlet)
-        return w, low, up, cy, cyu, cz, czu, w * dirichlet * g_at(j)
-
+        return w, low, up, cy, cyu, cz, czu, dirichlet
+
+    def thin_pass(terms, v, j, rhs):
+        w, low, up, cy, cyu, cz, czu, _ = terms[j]
+        d = v[j]
+        return (1.0 - RELAX) * d + w * (
+            rhs + low * v[j - 1] + up * v[j + 1]
+            + cy * roll(d, 1, 1) + cyu * roll(d, -1, 1) + cz * roll(d, 1, 0) + czu * roll(d, -1, 0)
+        )
+
+    def low_edge():
+        @pl.when(has_low)
+        def _():
+            e1_copy(2).wait_recv()
+            e1_copy(3).wait_recv()
+
+        press[1, 0] = pre[0] + axh[0] * (RELAX * e1a[0] / (e1b[0] + x_face(0)))
+        send_side(1, 0)
+
+    def up_edge():
+        @pl.when(has_up)
+        def _():
+            e1_copy(0).wait_recv()
+
+        x_up = e1a[1]
+        keep(top, RELAX / (d3[...] + x_up), raw(top), x_face(top), x_up)
+        edge_terms(0, 1)
+
+        @pl.when(has_up)
+        def _():
+            e1_copy(1).wait_recv()
+
+        press[1, top] = pre[1] + axh[1] * e1b[1]
+        send_side(1, 1)
+
+    inner_layer(0, 1)
+    edge_terms(0, 0)
+
+    @pl.when(last_x)
+    def _():
+        low_edge()
+
+    @pl.when(jnp.logical_not(last_x))
+    def _():
+        up_edge()
+
+    loads[4].wait()
+    loads[5].wait()
+
+    def wait_all(copies):
+        for copy in copies:
+            copy.wait_recv()
+
+    on_sides(lambda side: wait_all(thin_copies(1 - side)))
     terms = {j: thin_terms(j) for j in range(-2, layers + 2)}
-
-    def thin_pass(v, j):
-        w, low, up, cy, cyu, cz, czu, b = terms[j]
-        d = v[j]
-        return (1.0 - RELAX) * d + b + w * (
-            low * v[j - 1] + up * v[j + 1]
-            + cy * roll(d, 1, 1) + cyu * roll(d, -1, 1) + cz * roll(d, 1, 0) + czu * roll(d, -1, 0)
-        )
-
-    first = {j: terms[j][7] for j in range(-2, layers + 2)}
-    second = {j: thin_pass(first, j) for j in range(-1, layers + 1)}
-    third = {j: thin_pass(second, j) for j in range(layers)}
+    level = {j: terms[j][0] * thin_at(j, 3) for j in terms}
+    level = {j: thin_pass(terms, level, j, thin_at(j, 3)) for j in range(-1, layers + 1)}
+    level = {j: thin_pass(terms, level, j, thin_at(j, 3)) for j in range(layers)}
+    x_start(0, project(face_rows({l: terms[l][7] * level[l] for l in range(layers)})))
+
+    @pl.when(last_x)
+    def _():
+        up_edge()
+
+    @pl.when(jnp.logical_not(last_x))
+    def _():
+        low_edge()
+
+    inner_layer(0, top - 1)
+    forward(1)
+    x_finish(0)
+    z_start(0)
+
+    def one_pass(k, send):
+        for l in range(1, top):
+            inner_layer(k, l)
+        edge_terms(k, 0)
+        edge_terms(k, 1)
+        edges(k, send)
+
+    one_pass(1, True)
+    for l in range(layers):
+        near[l] = thinned(press[2, l])
+    on_sides(lambda side: near_copy(side).start())
+    for l in range(1, top):
+        inner_layer(2, l)
+    edge_terms(2, 0)
+    edge_terms(2, 1)
+    forward(2)
+    mortar = z_finish(0)
+    here = jnp.concatenate([mortar[i : i + 1, :] for i in range(rows_m)], axis=1)
+    under = jnp.concatenate([mortar[rows_m + i : rows_m + i + 1, :] for i in range(rows_m)], axis=1)
+
+    columns = zero_layer
+    for l in range(layers):
+        gb = jnp.sum(mb[l] * under, axis=1, keepdims=True)
+        gt = jnp.sum(mt[l] * here, axis=1, keepdims=True)
+        columns = jnp.where(iz == l, gb, columns)
+        columns = jnp.where(iz == layers + l, gt, columns)
+    g_own[...] = columns.T[0 : 2 * layers]
+    on_sides(lambda side: g_copy(side).start())
+
+    edges(2, True)
+    forward(3)
+    for l in range(1, top):
+        inner_layer(3, l)
+    edge_terms(3, 0)
+    edge_terms(3, 1)
+
+    on_sides(lambda side: near_copy(1 - side).wait_recv())
+    terms = {j: thin_terms(j) for j in range(-2, layers + 2)}
+    level = {j: near_low[j + 3] if j < 0 else near[j] if j < layers else near_up[j - layers] for j in range(-3, layers + 3)}
+    for width in (2, 1, 0):
+        level = {j: thin_pass(terms, level, j, thin_at(j, 3)) for j in range(-width, layers + width)}
+
+    on_sides(lambda side: g_copy(1 - side).wait_recv())
+
+    def g_at(j):
+        i = j % layers
+        ref = g_halo.at[0] if j < 0 else g_own if j < layers else g_halo.at[1]
+        return jnp.where(thin_row < 4, ref[i : i + 1, :], ref[layers + i : layers + i + 1, :])
+
+    given = {j: terms[j][7] * g_at(j) for j in terms}
+    extra = {j: terms[j][0] * given[j] for j in terms}
+    for width in (1, 0):
+        extra = {j: thin_pass(terms, extra, j, given[j]) for j in range(-width, layers + width)}
+    x_start(1, project(face_rows({l: terms[l][7] * (level[l] + extra[l] - g_at(l)) for l in range(layers)})))
 
     def added(l):
-        d = third[l]
+        d = extra[l]
         tall = jnp.concatenate(
             [jnp.where(thin_row < 4, d, 0.0), jnp.zeros((nz - 16, ny), F32), jnp.where(thin_row < 4, 0.0, d)], axis=0
         )
         return tall.T
 
-    def finish_layer(l):
-        p = press[5, l] + grid_d[l]
-        p_out[0, l] = p
-        return l, p
-
     for l in range(layers):
         grid_d[l] = added(l)
-    flux = project(no_flux, [finish_layer(l) for l in range(1, top)], True)
-    edges(4, False)
-    flux = project(flux, [finish_layer(l) for l in (0, top)], True)
-    x_start(1, flux)
+
+    edges(3, True)
     x_finish(1)
     z_start(1)
+    forward(4)
+    for l in range(1, top):
+        inner_layer(4, l)
+    edge_terms(4, 0)
+    edge_terms(4, 1)
+    for l in range(1, top):
+        p_out[0, l] = press[5, l] + grid_d[l]
+    edges(4, False)
+    for l in (0, top):
+        p_out[0, l] = press[5, l] + grid_d[l]
     final = mortar + z_finish(1)
     share = mort // sub_count
     offset = sub * share
@@ -635,7 +685,12 @@
     wide = jnp.broadcast_to(row, (8, 128))
     m_out[...] = pltpu.roll(wide, (128 - offset % 128) % 128, 1)[0:1, 0:share]
 
-    on_sides(lambda side: thin_copy(side).wait_send())
+    def sent_all(copies):
+        for copy in copies:
+            copy.wait_send()
+
+    on_sides(lambda side: sent_all(thin_copies(side)))
+    on_sides(lambda side: near_copy(side).wait_send())
     on_sides(lambda side: g_copy(side).wait_send())
 
     @pl.when(has_low)
@@ -712,19 +767,20 @@
         out_specs=(vmem, vmem),
         scratch_shapes=[
             field, field, field, field, basis, basis,
-            field, field, field, field, field, field, pair, field, field, field,
-            pltpu.VMEM((6, layers, ny, nz), F32), pair, field, field,
+            field, field, field, field, field, field, pair, field,
+            pltpu.VMEM((6, layers, ny, nz), F32), pair, field,
             pltpu.VMEM((ny, nz), F32), pair, pair, pltpu.VMEM((4, 2, ny, nz), F32),
             pltpu.VMEM((2, 8, 128), F32), pltpu.VMEM((2, xmsgs, 8, 128), F32),
             pltpu.VMEM((2, 8, 128), F32), pltpu.VMEM((2, zgroups - 1, 8, 128), F32),
             pltpu.VMEM((4, ny // GROUP, nz), F32), pltpu.VMEM((4, ny // CHUNKS, nz), F32),
-            pltpu.VMEM((layers, 3, 8, ny), F32), pltpu.VMEM((2, 3, 8, ny), F32), pltpu.VMEM((3, 3, 8, ny), F32),
+            pltpu.VMEM((layers, 4, 8, ny), F32), pltpu.VMEM((2, 4, 8, ny), F32), pltpu.VMEM((3, 4, 8, ny), F32),
+            pltpu.VMEM((layers, 8, ny), F32), pltpu.VMEM((3, 8, ny), F32), pltpu.VMEM((3, 8, ny), F32),
             pltpu.VMEM((2 * layers, ny), F32), pltpu.VMEM((2, 2 * layers, ny), F32),
             dma((6,)), dma((4,)), dma((4,)),
             dma((4, 2, CHUNKS)), dma((4, 2, CHUNKS)),
             dma((2, xmsgs)), dma((2, xmsgs)), dma((2, zgroups - 1)), dma((2, zgroups - 1)),
             dma((4,)), dma((4,)), dma((4,)), dma((4,)),
-            dma((2,)), dma((2,)), dma((2,)), dma((2,)),
+            dma((3,)), dma((3,)), dma((2,)), dma((2,)), dma((2,)), dma((2,)),
         ],
         compiler_params=pltpu.CompilerParams(collective_id=0, has_side_effects=True),
         name="mortar_darcy",

time: 76.8 us -> 67.3 us (0.88)
  the two profiles are of different devices: /device:TPU:64 before, /device:TPU:65 now
where the time goes in v3:
time: 67.3 us; the launch traced here: 67.1 us
  Pallas kernels  65.2 us (97%)
  local copies, waits for them, and re-layouts  1.22 us (2%)
    pallas_call x1, Pallas kernels, shards(): pl.pallas_call(functools.partial(kernel, sub_count, block_count), out_sha...  65.2 us

profile of v3, /device:TPU:65, one launch (start us, length us, event | category | flops | bytes accessed | tf_op | source)
XLA Modules:
  0.0 67.1 jit_solution(12601645397757909630)
XLA Ops:
  0.6 65.2 %mortar_darcy.1 = (f32[1,4,128,128]{3,2,1,0:T(8,128)S(1)}, f32[1,16]{1,0:T(1,128)S(1)}) custom-call(f32[1,4,128,128]{3,2,1,0:T(8,128)} %src_h.1, f32[1,4,128,128]{3,2,1,0:T(8,128)} %tx_h.1, f32[1,4,128,128]{3,2,1,0:T(8,128)} %ty_h.1, f32[1,4,128,128]{3,2,1,0:T(8,128)} %tz_h.1, f32[1,4,128,256]{3,2,1,0:T(8,128)} %mb_h.1, f32[1,4,128,256]{3,2,1,0:T(8,128)} %mt_h.1), custom_call_target="tpu_custom_call" | custom-call | tf_op jit(solution)/shard_map/mortar_darcy/pallas_call | solution.py:760
  65.9 0.7 %copy.10 = f32[1,4,128,128]{3,2,1,0:T(8,128)} copy(f32[1,4,128,128]{3,2,1,0:T(8,128)S(1)} %get-tuple-element.2) | data formatting | bytes 524288
  66.6 0.5 copy.11

commit v4 on v3

--- a/solution.py
+++ b/solution.py
@@ -26,7 +26,7 @@
     ayd, ayu, azd, azu, axd, axu, axh, bias, press, pre, grid_d,
     d3, e1a, e1b, halo, cbuf, xr, zs, zr, part1, part, thin, thin_low, thin_up, near, near_low, near_up, g_own, g_halo,
     load_sem, e1_send, e1_recv, h_send, h_recv, x_send, x_recv, z_send, z_recv,
-    p1_recv, f1_send, p_recv, f_send, t_send, t_recv, n_send, n_recv, g_send, g_recv,
+    p1_recv, f1_send, p_recv, f_send, t_send, t_recv, n_send, n_recv, g_send, g_recv, hello,
 ):
     layers, ny, nz = src.shape
     top = layers - 1
@@ -52,8 +52,9 @@
     loads = []
     for i, (h, v) in enumerate(((tx_h, tx), (ty_h, ty), (tz_h, tz), (src_h, src), (mb_h, mb), (mt_h, mt))):
         cp = pltpu.make_async_copy(h.at[0], v, load_sem.at[i])
-        cp.start()
         loads.append(cp)
+        if i < 4:
+            cp.start()
 
     barrier = pltpu.get_barrier_semaphore()
 
@@ -88,8 +89,14 @@
 
     for j in range(1, GROUP):
         greet(blk, xpeer(j))
-    for j in range(1, zgroups):
-        greet(blk, (zi + j) % zgroups * GROUP + xi)
+
+    @pl.when(group_low)
+    def _():
+        greet(blk, sub - GROUP)
+
+    @pl.when(group_up)
+    def _():
+        greet(blk, sub + GROUP)
 
     @pl.when(has_prev)
     def _():
@@ -102,7 +109,7 @@
             greet(blk + 1, xpeer(j))
 
     greeted = (
-        GROUP - 1 + zgroups - 1
+        GROUP - 1 + group_low.astype(jnp.int32) + group_up.astype(jnp.int32)
         + (GROUP - 1) * (slow_low.astype(jnp.int32) + slow_up.astype(jnp.int32))
         + pass_low.astype(jnp.int32) + pass_up.astype(jnp.int32)
         + GROUP * has_prev.astype(jnp.int32) + GROUP * has_next.astype(jnp.int32)
@@ -166,6 +173,8 @@
     loads[1].wait()
     loads[2].wait()
     loads[3].wait()
+    loads[4].start()
+    loads[5].start()
 
     def x_face(l):
         return tx[0] * low_mask if l == 0 else tx[l]
@@ -199,11 +208,14 @@
 
     parts3 = raw(top)
     d3[...] = x_face(top) + parts3[0] + parts3[1] + parts3[2] + parts3[3] + parts3[4]
-    for l in range(top):
+
+    def keep_low(l):
         parts = raw(l)
         low, up = x_face(l), tx[l + 1]
         diag = low + up + parts[0] + parts[1] + parts[2] + parts[3] + parts[4]
         keep(l, RELAX / diag, parts, low, up)
+
+    keep_low(0)
 
     thin_row = lax.broadcasted_iota(jnp.int32, (8, ny), 0)
     thin_y = lax.broadcasted_iota(jnp.int32, (8, ny), 1)
@@ -255,6 +267,31 @@
             copy.start()
 
     on_sides(lambda side: start_all(thin_copies(side)))
+
+    def on_groups(act):
+        @pl.when(group_low)
+        def _():
+            act(0)
+
+        @pl.when(group_up)
+        def _():
+            act(1)
+
+    def say_hello(r):
+        def one(side):
+            pl.semaphore_signal(
+                hello.at[r, 1 - side], inc=1, device_id={"block": blk, "sub": sub - GROUP + 2 * GROUP * side},
+                device_id_type=MESH,
+            )
+
+        if r < zgroups - 2:
+            on_groups(one)
+
+    def hear_hello(r):
+        if r < zgroups - 2:
+            on_groups(lambda side: pl.semaphore_wait(hello.at[r, side], 1))
+
+    say_hello(0)
 
     def e1_copy(i, rows=None):
         source_ref, dest_ref, step = (
@@ -311,6 +348,9 @@
             for i in pair:
                 e1_copy(i).start()
 
+    for l in range(1, top):
+        keep_low(l)
+
     for helps, pair in ((helps_low, (0, 1)), (helps_up, (2, 3))):
 
         @pl.when(helps)
@@ -594,6 +634,9 @@
         low_edge()
 
     inner_layer(0, top - 1)
+    for r in range(zgroups - 2):
+        hear_hello(r)
+        say_hello(r + 1)
     forward(1)
     x_finish(0)
     z_start(0)
@@ -628,11 +671,6 @@
     on_sides(lambda side: g_copy(side).start())
 
     edges(2, True)
-    forward(3)
-    for l in range(1, top):
-        inner_layer(3, l)
-    edge_terms(3, 0)
-    edge_terms(3, 1)
 
     on_sides(lambda side: near_copy(1 - side).wait_recv())
     terms = {j: thin_terms(j) for j in range(-2, layers + 2)}
@@ -663,9 +701,14 @@
     for l in range(layers):
         grid_d[l] = added(l)
 
-    edges(3, True)
+    for l in range(1, top):
+        inner_layer(3, l)
+    edge_terms(3, 0)
+    edge_terms(3, 1)
+    forward(3)
     x_finish(1)
     z_start(1)
+    edges(3, True)
     forward(4)
     for l in range(1, top):
         inner_layer(4, l)
@@ -781,6 +824,7 @@
             dma((2, xmsgs)), dma((2, xmsgs)), dma((2, zgroups - 1)), dma((2, zgroups - 1)),
             dma((4,)), dma((4,)), dma((4,)), dma((4,)),
             dma((3,)), dma((3,)), dma((2,)), dma((2,)), dma((2,)), dma((2,)),
+            pltpu.SemaphoreType.REGULAR((max(zgroups - 2, 1), 2)),
         ],
         compiler_params=pltpu.CompilerParams(collective_id=0, has_side_effects=True),
         name="mortar_darcy",

time: 67.3 us -> 63.9 us (0.949)
  the two profiles are of different devices: /device:TPU:65 before, /device:TPU:31 now
where the time goes in v4:
time: 63.9 us; the launch traced here: 63.8 us
  Pallas kernels  61.9 us (97%)
  local copies, waits for them, and re-layouts  1.22 us (2%)
  between operations  0.64 us (1%)
    pallas_call x1, Pallas kernels, shards(): pl.pallas_call(functools.partial(kernel, sub_count, block_count), out_sha...  61.9 us

profile of v4, /device:TPU:31, one launch (start us, length us, event | category | flops | bytes accessed | tf_op | source)
XLA Modules:
  0.0 63.8 jit_solution(6530014927636333538)
XLA Ops:
  0.6 61.9 %mortar_darcy.1 = (f32[1,4,128,128]{3,2,1,0:T(8,128)S(1)}, f32[1,16]{1,0:T(1,128)S(1)}) custom-call(f32[1,4,128,128]{3,2,1,0:T(8,128)} %src_h.1, f32[1,4,128,128]{3,2,1,0:T(8,128)} %tx_h.1, f32[1,4,128,128]{3,2,1,0:T(8,128)} %ty_h.1, f32[1,4,128,128]{3,2,1,0:T(8,128)} %tz_h.1, f32[1,4,128,256]{3,2,1,0:T(8,128)} %mb_h.1, f32[1,4,128,256]{3,2,1,0:T(8,128)} %mt_h.1), custom_call_target="tpu_custom_call" | custom-call | tf_op jit(solution)/shard_map/mortar_darcy/pallas_call | solution.py:803
  62.5 0.7 %copy.10 = f32[1,4,128,128]{3,2,1,0:T(8,128)} copy(f32[1,4,128,128]{3,2,1,0:T(8,128)S(1)} %get-tuple-element.2) | data formatting | bytes 524288
  63.2 0.5 copy.11

commit v5 on v4

--- a/solution.py
+++ b/solution.py
@@ -42,7 +42,11 @@
     has_prev = blk > 0
     has_next = blk < block_count - 1
     rows_c = ny // CHUNKS
-    rows_q = ny // GROUP
+    rows_q = (ny - 8) // (GROUP - 1)
+
+    def quarter(c):
+        return pl.ds(8 + (c - 1) * rows_q, rows_q)
+
     first_x = xi == 0
     last_x = xi == GROUP - 1
     group_low = zi > 0
@@ -90,7 +94,7 @@
     for j in range(1, GROUP):
         greet(blk, xpeer(j))
 
-    @pl.when(group_low)
+    @pl.when(group_low & jnp.logical_not(first_x))
     def _():
         greet(blk, sub - GROUP)
 
@@ -109,7 +113,7 @@
             greet(blk + 1, xpeer(j))
 
     greeted = (
-        GROUP - 1 + group_low.astype(jnp.int32) + group_up.astype(jnp.int32)
+        GROUP - 1 + group_low.astype(jnp.int32) + (group_up & jnp.logical_not(first_x)).astype(jnp.int32)
         + (GROUP - 1) * (slow_low.astype(jnp.int32) + slow_up.astype(jnp.int32))
         + pass_low.astype(jnp.int32) + pass_up.astype(jnp.int32)
         + GROUP * has_prev.astype(jnp.int32) + GROUP * has_next.astype(jnp.int32)
@@ -291,7 +295,6 @@
         if r < zgroups - 2:
             on_groups(lambda side: pl.semaphore_wait(hello.at[r, side], 1))
 
-    say_hello(0)
 
     def e1_copy(i, rows=None):
         source_ref, dest_ref, step = (
@@ -311,7 +314,7 @@
         source_ref = (tx.at[0], press.at[0, 0], d3, src.at[top])[i]
         helper = (xi + c) % GROUP if i >= 2 else (xi + GROUP - c) % GROUP
         return pltpu.make_async_remote_copy(
-            src_ref=source_ref.at[pl.ds(c * rows_q, rows_q)], dst_ref=part1.at[i],
+            src_ref=source_ref.at[quarter(c)], dst_ref=part1.at[i],
             send_sem=e1_send.at[i], recv_sem=p1_recv.at[i],
             device_id={"block": blk, "sub": zi * GROUP + helper}, device_id_type=MESH,
         )
@@ -323,7 +326,7 @@
         else:
             c, target = (GROUP - xi) % GROUP, (zi - 1) * GROUP + GROUP - 1
         return pltpu.make_async_remote_copy(
-            src_ref=part1.at[i], dst_ref=dest_ref.at[pl.ds(c * rows_q, rows_q)],
+            src_ref=part1.at[i], dst_ref=dest_ref.at[pl.ds(pl.multiple_of(8 + (c - 1) * rows_q, 8), rows_q)],
             send_sem=f1_send.at[i], recv_sem=e1_recv.at[i],
             device_id={"block": blk, "sub": target}, device_id_type=MESH,
         )
@@ -339,7 +342,7 @@
                 for i in pair:
                     e1_part(i, c).start()
             for i in pair:
-                e1_copy(i, pl.ds(0, rows_q)).start()
+                e1_copy(i, pl.ds(0, 8)).start()
 
     for beside, pair in ((jnp.logical_not(first_x), (0, 1)), (jnp.logical_not(last_x), (2, 3))):
 
@@ -607,9 +610,11 @@
     def _():
         low_edge()
 
-    @pl.when(jnp.logical_not(last_x))
+    @pl.when(first_x)
     def _():
         up_edge()
+
+    say_hello(0)
 
     loads[4].wait()
     loads[5].wait()
@@ -625,7 +630,7 @@
     level = {j: thin_pass(terms, level, j, thin_at(j, 3)) for j in range(layers)}
     x_start(0, project(face_rows({l: terms[l][7] * level[l] for l in range(layers)})))
 
-    @pl.when(last_x)
+    @pl.when(jnp.logical_not(first_x))
     def _():
         up_edge()
 
@@ -637,9 +642,9 @@
     for r in range(zgroups - 2):
         hear_hello(r)
         say_hello(r + 1)
-    forward(1)
     x_finish(0)
     z_start(0)
+    forward(1)
 
     def one_pass(k, send):
         for l in range(1, top):
@@ -670,7 +675,12 @@
     g_own[...] = columns.T[0 : 2 * layers]
     on_sides(lambda side: g_copy(side).start())
 
-    edges(2, True)
+    early = zi < 2
+
+    @pl.when(early)
+    def _():
+        edges(2, True)
+
 
     on_sides(lambda side: near_copy(1 - side).wait_recv())
     terms = {j: thin_terms(j) for j in range(-2, layers + 2)}
@@ -700,6 +710,10 @@
 
     for l in range(layers):
         grid_d[l] = added(l)
+
+    @pl.when(jnp.logical_not(early))
+    def _():
+        edges(2, True)
 
     for l in range(1, top):
         inner_layer(3, l)
@@ -815,7 +829,7 @@
             pltpu.VMEM((ny, nz), F32), pair, pair, pltpu.VMEM((4, 2, ny, nz), F32),
             pltpu.VMEM((2, 8, 128), F32), pltpu.VMEM((2, xmsgs, 8, 128), F32),
             pltpu.VMEM((2, 8, 128), F32), pltpu.VMEM((2, zgroups - 1, 8, 128), F32),
-            pltpu.VMEM((4, ny // GROUP, nz), F32), pltpu.VMEM((4, ny // CHUNKS, nz), F32),
+            pltpu.VMEM((4, (ny - 8) // (GROUP - 1), nz), F32), pltpu.VMEM((4, ny // CHUNKS, nz), F32),
             pltpu.VMEM((layers, 4, 8, ny), F32), pltpu.VMEM((2, 4, 8, ny), F32), pltpu.VMEM((3, 4, 8, ny), F32),
             pltpu.VMEM((layers, 8, ny), F32), pltpu.VMEM((3, 8, ny), F32), pltpu.VMEM((3, 8, ny), F32),
             pltpu.VMEM((2 * layers, ny), F32), pltpu.VMEM((2, 2 * layers, ny), F32),

time: 63.9 us -> 62.8 us (0.983)
  the two profiles are of different devices: /device:TPU:31 before, /device:TPU:30 now
where the time goes in v5:
time: 62.8 us; the launch traced here: 62.6 us
  Pallas kernels  60.8 us (97%)
  local copies, waits for them, and re-layouts  1.22 us (2%)
  between operations  0.64 us (1%)
    pallas_call x1, Pallas kernels, shards(): pl.pallas_call(functools.partial(kernel, sub_count, block_count), out_sha...  60.8 us

profile of v5, /device:TPU:30, one launch (start us, length us, event | category | flops | bytes accessed | tf_op | source)
XLA Modules:
  0.0 62.6 jit_solution(11171267399171353524)
XLA Ops:
  0.6 60.8 %mortar_darcy.1 = (f32[1,4,128,128]{3,2,1,0:T(8,128)S(1)}, f32[1,16]{1,0:T(1,128)S(1)}) custom-call(f32[1,4,128,128]{3,2,1,0:T(8,128)} %src_h.1, f32[1,4,128,128]{3,2,1,0:T(8,128)} %tx_h.1, f32[1,4,128,128]{3,2,1,0:T(8,128)} %ty_h.1, f32[1,4,128,128]{3,2,1,0:T(8,128)} %tz_h.1, f32[1,4,128,256]{3,2,1,0:T(8,128)} %mb_h.1, f32[1,4,128,256]{3,2,1,0:T(8,128)} %mt_h.1), custom_call_target="tpu_custom_call" | custom-call | tf_op jit(solution)/shard_map/mortar_darcy/pallas_call | solution.py:817
  61.4 0.7 %copy.10 = f32[1,4,128,128]{3,2,1,0:T(8,128)} copy(f32[1,4,128,128]{3,2,1,0:T(8,128)S(1)} %get-tuple-element.2) | data formatting | bytes 524288
  62.1 0.5 copy.11

commit v6 on v5

--- a/solution.py
+++ b/solution.py
@@ -624,6 +624,9 @@
             copy.wait_recv()
 
     on_sides(lambda side: wait_all(thin_copies(1 - side)))
+    for r in range(zgroups - 3):
+        hear_hello(r)
+        say_hello(r + 1)
     terms = {j: thin_terms(j) for j in range(-2, layers + 2)}
     level = {j: terms[j][0] * thin_at(j, 3) for j in terms}
     level = {j: thin_pass(terms, level, j, thin_at(j, 3)) for j in range(-1, layers + 1)}
@@ -639,9 +642,8 @@
         low_edge()
 
     inner_layer(0, top - 1)
-    for r in range(zgroups - 2):
-        hear_hello(r)
-        say_hello(r + 1)
+    if zgroups > 2:
+        hear_hello(zgroups - 3)
     x_finish(0)
     z_start(0)
     forward(1)

time: 62.8 us -> 62 us (0.987)
  the two profiles are of different devices: /device:TPU:30 before, /device:TPU:25 now
where the time goes in v6:
time: 62 us; the launch traced here: 61.9 us
  Pallas kernels  60 us (97%)
  local copies, waits for them, and re-layouts  1.22 us (2%)
  between operations  0.64 us (1%)
    pallas_call x1, Pallas kernels, shards(): pl.pallas_call(functools.partial(kernel, sub_count, block_count), out_sha...  60 us

profile of v6, /device:TPU:25, one launch (start us, length us, event | category | flops | bytes accessed | tf_op | source)
XLA Modules:
  0.0 61.9 jit_solution(2752722236031098569)
XLA Ops:
  0.6 60.0 %mortar_darcy.1 = (f32[1,4,128,128]{3,2,1,0:T(8,128)S(1)}, f32[1,16]{1,0:T(1,128)S(1)}) custom-call(f32[1,4,128,128]{3,2,1,0:T(8,128)} %src_h.1, f32[1,4,128,128]{3,2,1,0:T(8,128)} %tx_h.1, f32[1,4,128,128]{3,2,1,0:T(8,128)} %ty_h.1, f32[1,4,128,128]{3,2,1,0:T(8,128)} %tz_h.1, f32[1,4,128,256]{3,2,1,0:T(8,128)} %mb_h.1, f32[1,4,128,256]{3,2,1,0:T(8,128)} %mt_h.1), custom_call_target="tpu_custom_call" | custom-call | tf_op jit(solution)/shard_map/mortar_darcy/pallas_call | solution.py:819
  60.6 0.7 %copy.10 = f32[1,4,128,128]{3,2,1,0:T(8,128)} copy(f32[1,4,128,128]{3,2,1,0:T(8,128)S(1)} %get-tuple-element.2) | data formatting | bytes 524288
  61.3 0.5 copy.11
